TPU v7x, 128 devices: a whole 4x4x4 slice. The times are simulated.
128 devices in a mesh: gx: 8 (over z_lo, x), gy: 16 (over z_hi, y, core).
Axes of the slice: x: 4, y: 4, z: 4 (z_hi: 2, z_lo: 2; z = z_hi * 2 + z_lo), core: 2. Of those that a mesh axis runs over, the one named last changes fastest.
Arguments:
- e_field: float32 [3, 256, 512, 128], P(None, 'gx', 'gy'), may hold values from -6 to 6
- h_field: float32 [3, 256, 512, 128], P(None, 'gx', 'gy'), may hold values from -6 to 6
- psi: float32 [12, 256, 512, 128], P(None, 'gx', 'gy'), may hold values from -6 to 6
- material: int32 [256, 512, 128], P('gx', 'gy'), may hold values from 0 to 7
- eps_table: float32 [8], replicated, may hold values from 1 to 1.2
- sigma_table: float32 [8], replicated, may hold values from 0 to 0.05
Outputs:
- e_out: float32 [3, 256, 512, 128], P(None, 'gx', 'gy')
- h_out: float32 [3, 256, 512, 128], P(None, 'gx', 'gy')
- psi_out: float32 [12, 256, 512, 128], P(None, 'gx', 'gy')
All inputs are finite; a program needn't handle non-finite values.
Results may differ from a plain program's by a relative error of at most 0.0003.
Values sent between devices are 32-bit elements; how exact they have to be, the bound alone decides.
A program may use at most 128 MiB of HBM per device.

v0:
```python
import jax
import jax.numpy as jnp
from jax import lax
from jax.sharding import PartitionSpec as P

PML = 16
STEPS = 16
NMAT = 8


time_step = 0.5
sigma_peak = 3.0
kappa_peak = 5.0
alpha_peak = 0.05
rim_depth = 4
curl_table = (((2, 1), (1, 2)), ((0, 2), (2, 0)), ((1, 0), (0, 1)))


def with_halo(cells, sides, width):
    for axis, dim in sides:
        count = lax.axis_size(axis)
        ends = count - 1
        head = lax.slice_in_dim(cells, 0, width, axis=dim)
        tail = lax.slice_in_dim(cells, cells.shape[dim] - width, cells.shape[dim], axis=dim)
        cells = jnp.concatenate(
            [
                lax.ppermute(tail, axis, [(i, (i + 1) % count) for i in range(ends)]),
                cells,
                lax.ppermute(head, axis, [((i + 1) % count, i) for i in range(ends)]),
            ],
            axis=dim,
        )
    return cells


def profile(length, offset, extent, shift_half, thickness):
    position = (offset + lax.iota(jnp.int32, length)).astype(jnp.float32) + shift_half
    slab_width = jnp.float32(thickness)
    depth_frac = jnp.maximum(
        jnp.maximum(
            (slab_width - position) / slab_width, (position - (extent - slab_width)) / slab_width
        ),
        0.0,
    )
    depth_cube = depth_frac * depth_frac * depth_frac
    sigma_value = sigma_peak * depth_cube
    kappa_value = 1.0 + (kappa_peak - 1.0) * depth_cube
    alpha_value = alpha_peak * (1.0 - depth_frac)
    decays = jnp.exp(-(sigma_value / kappa_value + alpha_value) * time_step)
    scaling = (
        sigma_value * (decays - 1.0) / (kappa_value * (sigma_value + kappa_value * alpha_value))
    )
    inside_slab = depth_frac > 0.0
    return (
        jnp.where(inside_slab, decays, 0.0),
        jnp.where(inside_slab, scaling, 0.0),
        1.0 / kappa_value,
    )


def shaped(vector, direction):
    target_shape = [1, 1, 1]
    target_shape[direction] = vector.shape[0]
    return vector.reshape(target_shape)


def forward(field, direction, following):
    shifted = lax.slice_in_dim(field, 1, field.shape[direction], axis=direction)
    return jnp.concatenate([shifted, following], axis=direction) - field


def backward(field, direction, preceding):
    shifted = lax.slice_in_dim(field, 0, field.shape[direction] - 1, axis=direction)
    return field - jnp.concatenate([preceding, shifted], axis=direction)


def zero_layer(field, direction):
    return jnp.zeros_like(lax.slice_in_dim(field, 0, 1, axis=direction))


def plain_term(difference, auxiliary, coefficient, direction):
    decays, scaling, inverse = coefficient
    renewed = decays * auxiliary + scaling * difference
    return (inverse * difference + renewed, renewed)


def curl(difference_of, auxiliary, first_slot, coefficients, renew):
    results = []
    renewed_list = []
    for component in range(3):
        plus_pair, minus_pair = curl_table[component]
        slot = first_slot + 2 * component
        plus_value, plus_aux = renew(
            difference_of(plus_pair[0], plus_pair[1]),
            auxiliary[slot],
            coefficients[plus_pair[1]],
            plus_pair[1],
        )
        minus_value, minus_aux = renew(
            difference_of(minus_pair[0], minus_pair[1]),
            auxiliary[slot + 1],
            coefficients[minus_pair[1]],
            minus_pair[1],
        )
        results.append(plus_value - minus_value)
        renewed_list.append(plus_aux)
        renewed_list.append(minus_aux)
    return (results, renewed_list)


def material_coefficients(material, eps_table, sigma_table):
    losses = sigma_table * time_step / (2.0 * eps_table)
    keep_table = (1.0 - losses) / (1.0 + losses)
    drive_table = time_step / eps_table / (1.0 + losses)
    keeping = jnp.zeros(material.shape, jnp.float32)
    driving = jnp.zeros(material.shape, jnp.float32)
    for number in range(NMAT):
        chosen = material == number
        keeping = keeping + jnp.where(chosen, keep_table[number], 0.0)
        driving = driving + jnp.where(chosen, drive_table[number], 0.0)
    return (keeping, driving)


def profiles_for(layout):
    magnetic_coef = [
        tuple(
            (
                shaped(vector, direction)
                for vector in profile(
                    layout[direction][0], layout[direction][1], layout[direction][2], 0.5, PML
                )
            )
        )
        for direction in range(3)
    ]
    electric_coef = [
        tuple(
            (
                shaped(vector, direction)
                for vector in profile(
                    layout[direction][0], layout[direction][1], layout[direction][2], 0.0, PML
                )
            )
        )
        for direction in range(3)
    ]
    return (magnetic_coef, electric_coef)


def local_step(
    electric, magnetic, auxiliary, magnetic_coef, electric_coef, keeping, driving, renew, inside
):

    def electric_ahead(source, direction):
        field = electric[source]
        return forward(field, direction, zero_layer(field, direction))

    curl_h, renewed_h = curl(electric_ahead, auxiliary, 0, magnetic_coef, renew)
    magnetic_new = jnp.stack(
        [
            jnp.where(inside, magnetic[component] - time_step * curl_h[component], 0.0)
            for component in range(3)
        ]
    )

    def magnetic_behind(source, direction):
        field = magnetic_new[source]
        return backward(field, direction, zero_layer(field, direction))

    curl_e, renewed_e = curl(magnetic_behind, auxiliary, 6, electric_coef, renew)
    electric_new = jnp.stack(
        [
            jnp.where(inside, keeping * electric[component] + driving * curl_e[component], 0.0)
            for component in range(3)
        ]
    )
    return (electric_new, magnetic_new, jnp.stack(renewed_h + renewed_e))


def shards(e_field, h_field, psi, material, eps_table, sigma_table):
    rows_x = e_field.shape[1]
    rows_y = e_field.shape[2]
    depth_z = e_field.shape[3]
    extent_x = lax.axis_size("gx") * rows_x
    extent_y = lax.axis_size("gy") * rows_y
    start_x = lax.axis_index("gx") * rows_x - rim_depth
    start_y = lax.axis_index("gy") * rows_y - rim_depth
    wide_x = rows_x + 2 * rim_depth
    wide_y = rows_y + 2 * rim_depth
    layout = ((wide_x, start_x, extent_x), (wide_y, start_y, extent_y), (depth_z, 0, depth_z))
    magnetic_coef, electric_coef = profiles_for(layout)
    rim_material = with_halo(material, (("gx", 0), ("gy", 1)), rim_depth)
    keeping, driving = material_coefficients(rim_material, eps_table, sigma_table)
    place_x = start_x + lax.iota(jnp.int32, wide_x)
    place_y = start_y + lax.iota(jnp.int32, wide_y)
    inside_x = (place_x >= 0) & (place_x < extent_x)
    inside_y = (place_y >= 0) & (place_y < extent_y)
    inside = inside_x[:, None, None] & inside_y[None, :, None]

    def advance_block(turn_index, carry):
        electric, magnetic, auxiliary = carry
        stacked = jnp.concatenate([electric, magnetic, auxiliary], axis=0)
        widened = with_halo(stacked, (("gx", 1), ("gy", 2)), rim_depth)
        wide_electric = widened[0:3]
        wide_magnetic = widened[3:6]
        wide_auxiliary = widened[6:18]
        for inner_turn in range(rim_depth):
            wide_electric, wide_magnetic, wide_auxiliary = local_step(
                wide_electric,
                wide_magnetic,
                wide_auxiliary,
                magnetic_coef,
                electric_coef,
                keeping,
                driving,
                plain_term,
                inside,
            )
        return (
            wide_electric[:, rim_depth : rim_depth + rows_x, rim_depth : rim_depth + rows_y],
            wide_magnetic[:, rim_depth : rim_depth + rows_x, rim_depth : rim_depth + rows_y],
            wide_auxiliary[:, rim_depth : rim_depth + rows_x, rim_depth : rim_depth + rows_y],
        )

    e_out, h_out, psi_out = lax.fori_loop(
        0, STEPS // rim_depth, advance_block, (e_field, h_field, psi)
    )
    return (e_out, h_out, psi_out)


def solution(mesh):
    in_specs = (
        P(None, "gx", "gy", None),
        P(None, "gx", "gy", None),
        P(None, "gx", "gy", None),
        P("gx", "gy", None),
        P(),
        P(),
    )
    out_specs = (P(None, "gx", "gy", None), P(None, "gx", "gy", None), P(None, "gx", "gy", None))
    return jax.shard_map(shards, mesh=mesh, in_specs=in_specs, out_specs=out_specs, check_vma=False)
```

profile of v0, /device:TPU:96, one launch (start us, length us, event | category | flops | bytes accessed | tf_op | source)
XLA Modules:
  0.0 556.8 jit_solution(4052560447637098937)
XLA Ops:
  3.4 6.3 %copy.42 = f32[12,32,32,128]{3,2,1,0:T(8,128)} copy(f32[12,32,32,128]{3,2,1,0:T(8,128)} %param.10) | data formatting | bytes 12582912
  25.1 7.3 %collective-permute-done.6 = s32[40,4,128]{2,1,0:T(4,128)S(1)} collective-permute-done((s32[40,4,128]{2,1,0:T(4,128)S(1)}, s32[40,4,128]{2,1,0:T(4,128)S(1)}, u32[]{:S(2)}, u32[]{:S(2)}) %collective-permute-start.6) | collective-permute-done | bytes 81952 | tf_op jit(solution)/shard_map/ppermute | solution.py:27
  32.4 6.4 %select_add_fusion = (f32[40,40,128]{2,1,0:T(8,128)S(1)}, pred[40,40,128]{2,1,0:T(8,128)(4,1)S(1)}, pred[40,40,128]{2,1,0:T(8,128)(4,1)S(1)}, pred[40,40,128]{2,...) fusion(f32[]{:T(128)} %bitcast.15, f32[]{:T(128)} %bitcast.14, ...), kind=kLoop, calls=%fused_computation.261 | loop fusion | flops 5120000 | bytes 3276832 | tf_op jit(solution)/shard_map/add | solution.py:120
  44.6 511.1 %while.17 = (s32[]{:T(128)}, f32[3,32,32,128]{3,2,1,0:T(8,128)S(1)}, f32[3,32,32,128]{3,2,1,0:T(8,128)}, f32[12,32,32,128]{3,2,1,0:T(8,128)}, f32[40,40,128]{2,1...) while((s32[]{:T(128)}, ...), condition=%wide.region_1.2_spmd.clone.clone.clone, body=%wide.region_0.1_spmd.clone.clone.clone.sunk | while | flops 128403424 | bytes 539933952 | solution.py:225
  56.4 18.7 %collective-permute-done = f32[18,4,32,128]{3,2,1,0:T(8,128)S(1)} collective-permute-done((f32[18,4,32,128]{3,2,1,0:T(8,128)S(1)}, f32[18,4,32,128]{3,2,1,0:T(8,128)S(1)}, u32[]{:S(2)}, u32[]{:S(2)}) %collective-permute-start) | collective-permute-done | bytes 1179680 | tf_op jit(solution)/shard_map/while/body/eval_jaxpr/ppermute | solution.py:29
  83.8 6.4 %collective-permute-start.2 = (f32[18,40,4,128]{3,2,1,0:T(4,128)}, f32[18,40,4,128]{3,2,1,0:T(4,128)}, u32[]{:S(2)}, u32[]{:S(2)}) collective-permute-start(f32[18,40,4,128]{3,2,1,0:T(4,128)} %get-tuple-element.698), channel_id=1, source_target_pairs={{1,0},{2,1},{3,2},{4,3},{5,4},{6,5},{7,6},{8,7},{9,8},{10,9},{11,1... | collective-permute-start | bytes 4423688 | tf_op jit(solution)/shard_map/while/body/eval_jaxpr/ppermute | solution.py:29
  92.5 14.9 %collective-permute-done.2 = f32[18,40,4,128]{3,2,1,0:T(4,128)} collective-permute-done((f32[18,40,4,128]{3,2,1,0:T(4,128)}, f32[18,40,4,128]{3,2,1,0:T(4,128)}, u32[]{:S(2)}, u32[]{:S(2)}) %collective-permute-start.2) | collective-permute-done | bytes 1474592 | tf_op jit(solution)/shard_map/while/body/eval_jaxpr/ppermute | solution.py:29
  107.4 7.4 %collective-permute-done.3 = f32[18,40,4,128]{3,2,1,0:T(4,128)} collective-permute-done((f32[18,40,4,128]{3,2,1,0:T(4,128)}, f32[18,40,4,128]{3,2,1,0:T(4,128)}, u32[]{:S(2)}, u32[]{:S(2)}) %collective-permute-start.3) | collective-permute-done | bytes 1474592 | tf_op jit(solution)/shard_map/while/body/eval_jaxpr/ppermute | solution.py:27
  169.3 7.0 %slice.933 = f32[12,32,32,128]{3,2,1,0:T(8,128)} slice(f32[12,40,40,128]{3,2,1,0:T(8,128)} %bitcast_dynamic-update-slice_fusion.35), slice={[0:12], [4:36], [4:36], [0:128]} | slice | bytes 12582912 | tf_op jit(solution)/shard_map/while/body/eval_jaxpr/slice | solution.py:222
  188.2 15.0 %collective-permute-done = f32[18,4,32,128]{3,2,1,0:T(8,128)S(1)} collective-permute-done((f32[18,4,32,128]{3,2,1,0:T(8,128)S(1)}, f32[18,4,32,128]{3,2,1,0:T(8,128)S(1)}, u32[]{:S(2)}, u32[]{:S(2)}) %collective-permute-start) | collective-permute-done | bytes 1179680 | tf_op jit(solution)/shard_map/while/body/eval_jaxpr/ppermute | solution.py:29
  209.6 7.9 %collective-permute-start.2 = (f32[18,40,4,128]{3,2,1,0:T(4,128)}, f32[18,40,4,128]{3,2,1,0:T(4,128)}, u32[]{:S(2)}, u32[]{:S(2)}) collective-permute-start(f32[18,40,4,128]{3,2,1,0:T(4,128)} %get-tuple-element.698), channel_id=1, source_target_pairs={{1,0},{2,1},{3,2},{4,3},{5,4},{6,5},{7,6},{8,7},{9,8},{10,9},{11,1... | collective-permute-start | bytes 4423688 | tf_op jit(solution)/shard_map/while/body/eval_jaxpr/ppermute | solution.py:29
  219.8 14.9 %collective-permute-done.2 = f32[18,40,4,128]{3,2,1,0:T(4,128)} collective-permute-done((f32[18,40,4,128]{3,2,1,0:T(4,128)}, f32[18,40,4,128]{3,2,1,0:T(4,128)}, u32[]{:S(2)}, u32[]{:S(2)}) %collective-permute-start.2) | collective-permute-done | bytes 1474592 | tf_op jit(solution)/shard_map/while/body/eval_jaxpr/ppermute | solution.py:29
  234.7 7.4 %collective-permute-done.3 = f32[18,40,4,128]{3,2,1,0:T(4,128)} collective-permute-done((f32[18,40,4,128]{3,2,1,0:T(4,128)}, f32[18,40,4,128]{3,2,1,0:T(4,128)}, u32[]{:S(2)}, u32[]{:S(2)}) %collective-permute-start.3) | collective-permute-done | bytes 1474592 | tf_op jit(solution)/shard_map/while/body/eval_jaxpr/ppermute | solution.py:27
  296.6 7.0 %slice.933 = f32[12,32,32,128]{3,2,1,0:T(8,128)} slice(f32[12,40,40,128]{3,2,1,0:T(8,128)} %bitcast_dynamic-update-slice_fusion.35), slice={[0:12], [4:36], [4:36], [0:128]} | slice | bytes 12582912 | tf_op jit(solution)/shard_map/while/body/eval_jaxpr/slice | solution.py:222
  315.4 13.2 %collective-permute-done = f32[18,4,32,128]{3,2,1,0:T(8,128)S(1)} collective-permute-done((f32[18,4,32,128]{3,2,1,0:T(8,128)S(1)}, f32[18,4,32,128]{3,2,1,0:T(8,128)S(1)}, u32[]{:S(2)}, u32[]{:S(2)}) %collective-permute-start) | collective-permute-done | bytes 1179680 | tf_op jit(solution)/shard_map/while/body/eval_jaxpr/ppermute | solution.py:29
  335.1 8.2 %collective-permute-start.2 = (f32[18,40,4,128]{3,2,1,0:T(4,128)}, f32[18,40,4,128]{3,2,1,0:T(4,128)}, u32[]{:S(2)}, u32[]{:S(2)}) collective-permute-start(f32[18,40,4,128]{3,2,1,0:T(4,128)} %get-tuple-element.698), channel_id=1, source_target_pairs={{1,0},{2,1},{3,2},{4,3},{5,4},{6,5},{7,6},{8,7},{9,8},{10,9},{11,1... | collective-permute-start | bytes 4423688 | tf_op jit(solution)/shard_map/while/body/eval_jaxpr/ppermute | solution.py:29
  345.7 14.9 %collective-permute-done.2 = f32[18,40,4,128]{3,2,1,0:T(4,128)} collective-permute-done((f32[18,40,4,128]{3,2,1,0:T(4,128)}, f32[18,40,4,128]{3,2,1,0:T(4,128)}, u32[]{:S(2)}, u32[]{:S(2)}) %collective-permute-start.2) | collective-permute-done | bytes 1474592 | tf_op jit(solution)/shard_map/while/body/eval_jaxpr/ppermute | solution.py:29
  360.6 7.4 %collective-permute-done.3 = f32[18,40,4,128]{3,2,1,0:T(4,128)} collective-permute-done((f32[18,40,4,128]{3,2,1,0:T(4,128)}, f32[18,40,4,128]{3,2,1,0:T(4,128)}, u32[]{:S(2)}, u32[]{:S(2)}) %collective-permute-start.3) | collective-permute-done | bytes 1474592 | tf_op jit(solution)/shard_map/while/body/eval_jaxpr/ppermute | solution.py:27
  422.4 7.0 %slice.933 = f32[12,32,32,128]{3,2,1,0:T(8,128)} slice(f32[12,40,40,128]{3,2,1,0:T(8,128)} %bitcast_dynamic-update-slice_fusion.35), slice={[0:12], [4:36], [4:36], [0:128]} | slice | bytes 12582912 | tf_op jit(solution)/shard_map/while/body/eval_jaxpr/slice | solution.py:222
  441.3 12.2 %collective-permute-done = f32[18,4,32,128]{3,2,1,0:T(8,128)S(1)} collective-permute-done((f32[18,4,32,128]{3,2,1,0:T(8,128)S(1)}, f32[18,4,32,128]{3,2,1,0:T(8,128)S(1)}, u32[]{:S(2)}, u32[]{:S(2)}) %collective-permute-start) | collective-permute-done | bytes 1179680 | tf_op jit(solution)/shard_map/while/body/eval_jaxpr/ppermute | solution.py:29
  460.0 8.0 %collective-permute-start.2 = (f32[18,40,4,128]{3,2,1,0:T(4,128)}, f32[18,40,4,128]{3,2,1,0:T(4,128)}, u32[]{:S(2)}, u32[]{:S(2)}) collective-permute-start(f32[18,40,4,128]{3,2,1,0:T(4,128)} %get-tuple-element.698), channel_id=1, source_target_pairs={{1,0},{2,1},{3,2},{4,3},{5,4},{6,5},{7,6},{8,7},{9,8},{10,9},{11,1... | collective-permute-start | bytes 4423688 | tf_op jit(solution)/shard_map/while/body/eval_jaxpr/ppermute | solution.py:29
  470.3 14.9 %collective-permute-done.2 = f32[18,40,4,128]{3,2,1,0:T(4,128)} collective-permute-done((f32[18,40,4,128]{3,2,1,0:T(4,128)}, f32[18,40,4,128]{3,2,1,0:T(4,128)}, u32[]{:S(2)}, u32[]{:S(2)}) %collective-permute-start.2) | collective-permute-done | bytes 1474592 | tf_op jit(solution)/shard_map/while/body/eval_jaxpr/ppermute | solution.py:29
  485.2 7.4 %collective-permute-done.3 = f32[18,40,4,128]{3,2,1,0:T(4,128)} collective-permute-done((f32[18,40,4,128]{3,2,1,0:T(4,128)}, f32[18,40,4,128]{3,2,1,0:T(4,128)}, u32[]{:S(2)}, u32[]{:S(2)}) %collective-permute-start.3) | collective-permute-done | bytes 1474592 | tf_op jit(solution)/shard_map/while/body/eval_jaxpr/ppermute | solution.py:27
  547.1 7.0 %slice.933 = f32[12,32,32,128]{3,2,1,0:T(8,128)} slice(f32[12,40,40,128]{3,2,1,0:T(8,128)} %bitcast_dynamic-update-slice_fusion.35), slice={[0:12], [4:36], [4:36], [0:128]} | slice | bytes 12582912 | tf_op jit(solution)/shard_map/while/body/eval_jaxpr/slice | solution.py:222
  (513 shorter events, 326.4 us)
Async XLA Ops:
  3.4 41.2 %copy-start.15 = (f32[3,32,32,128]{3,2,1,0:T(8,128)S(1)}, f32[3,32,32,128]{3,2,1,0:T(8,128)}, u32[]{:S(2)}) copy-start(f32[3,32,32,128]{3,2,1,0:T(8,128)} %param.8) | copy-start | bytes 4718596
  9.7 9.4 %collective-permute-start.4 = (s32[4,32,128]{2,1,0:T(8,128)S(1)}, s32[4,32,128]{2,1,0:T(8,128)S(1)}, u32[]{:S(2)}, u32[]{:S(2)}) collective-permute-start(s32[4,32,128]{2,1,0:T(8,128)S(1)} %get-tuple-element.562), channel_id=1, source_target_pairs={{0,16},{16,32},{32,48},{48,64},{64,80},{80,96},{96,112},{1,17},{17... | collective-permute-start | bytes 196616 | tf_op jit(solution)/shard_map/ppermute | solution.py:27
  13.1 6.4 %collective-permute-start.5 = (s32[4,32,128]{2,1,0:T(8,128)S(1)}, s32[4,32,128]{2,1,0:T(8,128)S(1)}, u32[]{:S(2)}, u32[]{:S(2)}) collective-permute-start(s32[4,32,128]{2,1,0:T(8,128)S(1)} %get-tuple-element.561), channel_id=1, source_target_pairs={{16,0},{32,16},{48,32},{64,48},{80,64},{96,80},{112,96},{17,1},{33... | collective-permute-start | bytes 196616 | tf_op jit(solution)/shard_map/ppermute | solution.py:29
  19.6 5.5 collective-permute-start.7
  23.0 9.4 %collective-permute-start.6 = (s32[40,4,128]{2,1,0:T(4,128)S(1)}, s32[40,4,128]{2,1,0:T(4,128)S(1)}, u32[]{:S(2)}, u32[]{:S(2)}) collective-permute-start(s32[40,4,128]{2,1,0:T(4,128)S(1)} %get-tuple-element.559), channel_id=1, source_target_pairs={{0,1},{1,2},{2,3},{3,4},{4,5},{5,6},{6,7},{7,8},{8,9},{9,10},{10,1... | collective-permute-start | bytes 245768 | tf_op jit(solution)/shard_map/ppermute | solution.py:27
  48.8 35.0 %copy-start = (f32[18,32,32,128]{3,2,1,0:T(8,128)}, f32[18,32,32,128]{3,2,1,0:T(8,128)S(1)}, u32[]{:S(2)}) copy-start(f32[18,32,32,128]{3,2,1,0:T(8,128)S(1)} %constant_dynamic-update-slice_fusion.11) | copy-start | bytes 28311556 | tf_op jit(solution)/shard_map/while
  49.2 26.0 %collective-permute-start = (f32[18,4,32,128]{3,2,1,0:T(8,128)S(1)}, f32[18,4,32,128]{3,2,1,0:T(8,128)S(1)}, u32[]{:S(2)}, u32[]{:S(2)}) collective-permute-start(f32[18,4,32,128]{3,2,1,0:T(8,128)S(1)} %get-tuple-element.696), channel_id=1, source_target_pairs={{16,0},{32,16},{48,32},{64,48},{80,64},{96,80},{112,96},{17,1},{33... | collective-permute-start | bytes 3538952 | tf_op jit(solution)/shard_map/while/body/eval_jaxpr/ppermute | solution.py:29
  54.5 26.9 %collective-permute-start.1 = (f32[18,4,32,128]{3,2,1,0:T(8,128)S(1)}, f32[18,4,32,128]{3,2,1,0:T(8,128)S(1)}, u32[]{:S(2)}, u32[]{:S(2)}) collective-permute-start(f32[18,4,32,128]{3,2,1,0:T(8,128)S(1)} %get-tuple-element.697), channel_id=1, source_target_pairs={{0,16},{16,32},{32,48},{48,64},{64,80},{80,96},{96,112},{1,17},{17... | collective-permute-start | bytes 3538952 | tf_op jit(solution)/shard_map/while/body/eval_jaxpr/ppermute | solution.py:27
  83.8 23.6 %collective-permute-start.2 = (f32[18,40,4,128]{3,2,1,0:T(4,128)}, f32[18,40,4,128]{3,2,1,0:T(4,128)}, u32[]{:S(2)}, u32[]{:S(2)}) collective-permute-start(f32[18,40,4,128]{3,2,1,0:T(4,128)} %get-tuple-element.698), channel_id=1, source_target_pairs={{1,0},{2,1},{3,2},{4,3},{5,4},{6,5},{7,6},{8,7},{9,8},{10,9},{11,1... | collective-permute-start | bytes 4423688 | tf_op jit(solution)/shard_map/while/body/eval_jaxpr/ppermute | solution.py:29
  90.2 24.6 %collective-permute-start.3 = (f32[18,40,4,128]{3,2,1,0:T(4,128)}, f32[18,40,4,128]{3,2,1,0:T(4,128)}, u32[]{:S(2)}, u32[]{:S(2)}) collective-permute-start(f32[18,40,4,128]{3,2,1,0:T(4,128)} %get-tuple-element.699), channel_id=1, source_target_pairs={{0,1},{1,2},{2,3},{3,4},{4,5},{5,6},{6,7},{7,8},{8,9},{9,10},{10,1... | collective-permute-start | bytes 4423688 | tf_op jit(solution)/shard_map/while/body/eval_jaxpr/ppermute | solution.py:27
  182.0 27.6 %copy-start = (f32[18,32,32,128]{3,2,1,0:T(8,128)}, f32[18,32,32,128]{3,2,1,0:T(8,128)S(1)}, u32[]{:S(2)}) copy-start(f32[18,32,32,128]{3,2,1,0:T(8,128)S(1)} %constant_dynamic-update-slice_fusion.11) | copy-start | bytes 28311556 | tf_op jit(solution)/shard_map/while
  182.3 20.8 %collective-permute-start = (f32[18,4,32,128]{3,2,1,0:T(8,128)S(1)}, f32[18,4,32,128]{3,2,1,0:T(8,128)S(1)}, u32[]{:S(2)}, u32[]{:S(2)}) collective-permute-start(f32[18,4,32,128]{3,2,1,0:T(8,128)S(1)} %get-tuple-element.696), channel_id=1, source_target_pairs={{16,0},{32,16},{48,32},{64,48},{80,64},{96,80},{112,96},{17,1},{33... | collective-permute-start | bytes 3538952 | tf_op jit(solution)/shard_map/while/body/eval_jaxpr/ppermute | solution.py:29
  184.2 22.9 %collective-permute-start.1 = (f32[18,4,32,128]{3,2,1,0:T(8,128)S(1)}, f32[18,4,32,128]{3,2,1,0:T(8,128)S(1)}, u32[]{:S(2)}, u32[]{:S(2)}) collective-permute-start(f32[18,4,32,128]{3,2,1,0:T(8,128)S(1)} %get-tuple-element.697), channel_id=1, source_target_pairs={{0,16},{16,32},{32,48},{48,64},{64,80},{80,96},{96,112},{1,17},{17... | collective-permute-start | bytes 3538952 | tf_op jit(solution)/shard_map/while/body/eval_jaxpr/ppermute | solution.py:27
  209.6 25.1 %collective-permute-start.2 = (f32[18,40,4,128]{3,2,1,0:T(4,128)}, f32[18,40,4,128]{3,2,1,0:T(4,128)}, u32[]{:S(2)}, u32[]{:S(2)}) collective-permute-start(f32[18,40,4,128]{3,2,1,0:T(4,128)} %get-tuple-element.698), channel_id=1, source_target_pairs={{1,0},{2,1},{3,2},{4,3},{5,4},{6,5},{7,6},{8,7},{9,8},{10,9},{11,1... | collective-permute-start | bytes 4423688 | tf_op jit(solution)/shard_map/while/body/eval_jaxpr/ppermute | solution.py:29
  217.5 24.6 %collective-permute-start.3 = (f32[18,40,4,128]{3,2,1,0:T(4,128)}, f32[18,40,4,128]{3,2,1,0:T(4,128)}, u32[]{:S(2)}, u32[]{:S(2)}) collective-permute-start(f32[18,40,4,128]{3,2,1,0:T(4,128)} %get-tuple-element.699), channel_id=1, source_target_pairs={{0,1},{1,2},{2,3},{3,4},{4,5},{5,6},{6,7},{7,8},{8,9},{9,10},{10,1... | collective-permute-start | bytes 4423688 | tf_op jit(solution)/shard_map/while/body/eval_jaxpr/ppermute | solution.py:27
  309.2 25.9 %copy-start = (f32[18,32,32,128]{3,2,1,0:T(8,128)}, f32[18,32,32,128]{3,2,1,0:T(8,128)S(1)}, u32[]{:S(2)}) copy-start(f32[18,32,32,128]{3,2,1,0:T(8,128)S(1)} %constant_dynamic-update-slice_fusion.11) | copy-start | bytes 28311556 | tf_op jit(solution)/shard_map/while
  309.6 19.1 %collective-permute-start = (f32[18,4,32,128]{3,2,1,0:T(8,128)S(1)}, f32[18,4,32,128]{3,2,1,0:T(8,128)S(1)}, u32[]{:S(2)}, u32[]{:S(2)}) collective-permute-start(f32[18,4,32,128]{3,2,1,0:T(8,128)S(1)} %get-tuple-element.696), channel_id=1, source_target_pairs={{16,0},{32,16},{48,32},{64,48},{80,64},{96,80},{112,96},{17,1},{33... | collective-permute-start | bytes 3538952 | tf_op jit(solution)/shard_map/while/body/eval_jaxpr/ppermute | solution.py:29
  311.5 21.2 %collective-permute-start.1 = (f32[18,4,32,128]{3,2,1,0:T(8,128)S(1)}, f32[18,4,32,128]{3,2,1,0:T(8,128)S(1)}, u32[]{:S(2)}, u32[]{:S(2)}) collective-permute-start(f32[18,4,32,128]{3,2,1,0:T(8,128)S(1)} %get-tuple-element.697), channel_id=1, source_target_pairs={{0,16},{16,32},{32,48},{48,64},{64,80},{80,96},{96,112},{1,17},{17... | collective-permute-start | bytes 3538952 | tf_op jit(solution)/shard_map/while/body/eval_jaxpr/ppermute | solution.py:27
  335.1 25.4 %collective-permute-start.2 = (f32[18,40,4,128]{3,2,1,0:T(4,128)}, f32[18,40,4,128]{3,2,1,0:T(4,128)}, u32[]{:S(2)}, u32[]{:S(2)}) collective-permute-start(f32[18,40,4,128]{3,2,1,0:T(4,128)} %get-tuple-element.698), channel_id=1, source_target_pairs={{1,0},{2,1},{3,2},{4,3},{5,4},{6,5},{7,6},{8,7},{9,8},{10,9},{11,1... | collective-permute-start | bytes 4423688 | tf_op jit(solution)/shard_map/while/body/eval_jaxpr/ppermute | solution.py:29
  343.4 24.6 %collective-permute-start.3 = (f32[18,40,4,128]{3,2,1,0:T(4,128)}, f32[18,40,4,128]{3,2,1,0:T(4,128)}, u32[]{:S(2)}, u32[]{:S(2)}) collective-permute-start(f32[18,40,4,128]{3,2,1,0:T(4,128)} %get-tuple-element.699), channel_id=1, source_target_pairs={{0,1},{1,2},{2,3},{3,4},{4,5},{5,6},{6,7},{7,8},{8,9},{9,10},{10,1... | collective-permute-start | bytes 4423688 | tf_op jit(solution)/shard_map/while/body/eval_jaxpr/ppermute | solution.py:27
  435.5 18.1 %collective-permute-start = (f32[18,4,32,128]{3,2,1,0:T(8,128)S(1)}, f32[18,4,32,128]{3,2,1,0:T(8,128)S(1)}, u32[]{:S(2)}, u32[]{:S(2)}) collective-permute-start(f32[18,4,32,128]{3,2,1,0:T(8,128)S(1)} %get-tuple-element.696), channel_id=1, source_target_pairs={{16,0},{32,16},{48,32},{64,48},{80,64},{96,80},{112,96},{17,1},{33... | collective-permute-start | bytes 3538952 | tf_op jit(solution)/shard_map/while/body/eval_jaxpr/ppermute | solution.py:29
  437.4 20.2 %collective-permute-start.1 = (f32[18,4,32,128]{3,2,1,0:T(8,128)S(1)}, f32[18,4,32,128]{3,2,1,0:T(8,128)S(1)}, u32[]{:S(2)}, u32[]{:S(2)}) collective-permute-start(f32[18,4,32,128]{3,2,1,0:T(8,128)S(1)} %get-tuple-element.697), channel_id=1, source_target_pairs={{0,16},{16,32},{32,48},{48,64},{64,80},{80,96},{96,112},{1,17},{17... | collective-permute-start | bytes 3538952 | tf_op jit(solution)/shard_map/while/body/eval_jaxpr/ppermute | solution.py:27
  460.0 25.2 %collective-permute-start.2 = (f32[18,40,4,128]{3,2,1,0:T(4,128)}, f32[18,40,4,128]{3,2,1,0:T(4,128)}, u32[]{:S(2)}, u32[]{:S(2)}) collective-permute-start(f32[18,40,4,128]{3,2,1,0:T(4,128)} %get-tuple-element.698), channel_id=1, source_target_pairs={{1,0},{2,1},{3,2},{4,3},{5,4},{6,5},{7,6},{8,7},{9,8},{10,9},{11,1... | collective-permute-start | bytes 4423688 | tf_op jit(solution)/shard_map/while/body/eval_jaxpr/ppermute | solution.py:29
  468.0 24.6 %collective-permute-start.3 = (f32[18,40,4,128]{3,2,1,0:T(4,128)}, f32[18,40,4,128]{3,2,1,0:T(4,128)}, u32[]{:S(2)}, u32[]{:S(2)}) collective-permute-start(f32[18,40,4,128]{3,2,1,0:T(4,128)} %get-tuple-element.699), channel_id=1, source_target_pairs={{0,1},{1,2},{2,3},{3,4},{4,5},{5,6},{6,7},{7,8},{8,9},{9,10},{10,1... | collective-permute-start | bytes 4423688 | tf_op jit(solution)/shard_map/while/body/eval_jaxpr/ppermute | solution.py:27
  (65 other events, 271.8 us)
where the time goes:
time: 558 us; the launch traced here: 557 us
  other arithmetic  223 us (40%)
  waiting for transfers between devices  175 us (31%)
  local copies, waits for them, and re-layouts  78.8 us (14%)
  starting transfers between devices  76.3 us (14%)
    ppermute x10, waiting for transfers between devices, with_halo(): lax.ppermute(head, axis, [((i + 1) % count, i) for i in range(ends)])  119 us
    ppermute x10, waiting for transfers between devices, with_halo(): lax.ppermute(tail, axis, [(i, (i + 1) % count) for i in range(ends)])  55.4 us
    select_n x36, other arithmetic, local_step(): jnp.where(inside, keeping * electric[component] + driving * curl_e[compon...  52.6 us
    while x44, other arithmetic  50.4 us
    ppermute x10, starting transfers between devices, with_halo(): lax.ppermute(head, axis, [((i + 1) % count, i) for i in range(ends)])  49.6 us
    select_n x48, other arithmetic, local_step(): jnp.where(inside, magnetic[component] - time_step * curl_h[component], 0.0)  49.5 us
    slice x4, local copies, waits for them, and re-layouts, advance_block(): wide_auxiliary[:, rim_depth:rim_depth + rows_x, rim_depth:rim_depth + row...  27.8 us
    ppermute x10, starting transfers between devices, with_halo(): lax.ppermute(tail, axis, [(i, (i + 1) % count) for i in range(ends)])  26.7 us
  transfers between devices with their start and end apart: 20, of which 19 were waited for; matrix products, arithmetic and copies ran while one was open for 0% of the time, Pallas kernels for 0%

commit v1 on v0

v1 whole, which is shorter than its diff:
```python
import functools

import jax
import jax.numpy as jnp
from jax import lax
from jax.experimental import pallas as pl
from jax.experimental.pallas import tpu as pltpu
from jax.sharding import PartitionSpec as P

PML = 16
STEPS = 16
NMAT = 8
time_step = 0.5
sigma_peak = 3.0
kappa_peak = 5.0
alpha_peak = 0.05

M = 4
XO, XR = 5, 42
YO, YP = 8, 48
PYP = 24
U = 4
NA = 7
Z_SLOTS = (1, 2, 7, 8)
X_SLOTS = (3, 4, 9, 10)
Y_SLOTS = (0, 5, 6, 11)
MESH = pl.DeviceIdType.MESH
DIRS = ((-1, 0), (1, 0), (0, -1), (0, 1), (-1, -1), (-1, 1), (1, -1), (1, 1))
OPP = (1, 0, 3, 2, 7, 6, 5, 4)
LAYER = NA * 32
FACE = M * LAYER
CORNER = NA * M * M
EDGE = M * 4 * 16


def profile_of(position, extent):
    width = jnp.float32(PML)
    depth = jnp.maximum(
        jnp.maximum((width - position) / width, (position - (extent - width)) / width), 0.0
    )
    cube = depth * depth * depth
    sigma = sigma_peak * cube
    kappa = 1.0 + (kappa_peak - 1.0) * cube
    alpha = alpha_peak * (1.0 - depth)
    b = jnp.exp(-(sigma / kappa + alpha) * time_step)
    a = sigma * (b - 1.0) / (kappa * (sigma + kappa * alpha))
    inside = depth > 0.0
    return jnp.where(inside, b, 0.0), jnp.where(inside, a, 0.0), 1.0 / kappa


def kernel(nx, ny, e_in, h_in, psi_in, mat_in, eps_in, sig_in, e_out, h_out, psi_out, *scratch):
    scratch = list(scratch)
    take = lambda n: [scratch.pop(0) for _ in range(n)]
    E, H, PZ, PX, PY = take(3), take(3), take(4), take(4), take(4)
    KP, DR, MF, MI, ZB = take(5)
    xtab, ytab, ztab = take(1)[0], take(1)[0], take(1)[0]
    send_f, recv_f = take(4), take(4)
    send_c, recv_c = take(4), take(4)
    send_e, recv_e = take(4), take(4)
    send_m, recv_m = take(4), take(4)
    send_mc, recv_mc = take(4), take(4)
    in_sem, out_sem, zero_sem, s_sem, r_sem, sm_sem, rm_sem = take(7)

    gx, gy = lax.axis_index("gx"), lax.axis_index("gy")
    zero = jnp.minimum(gx, 0)
    x_first, x_last = gx == 0, gx == nx - 1
    y_first, y_last = gy == 0, gy == ny - 1
    x_edge = jnp.logical_or(x_first, x_last)
    y_edge = jnp.logical_or(y_first, y_last)
    exists = []
    for dx, dy in DIRS:
        ok = None
        for delta, first, last in ((dx, x_first, x_last), (dy, y_first, y_last)):
            if delta:
                here = jnp.logical_not(first if delta < 0 else last)
                ok = here if ok is None else jnp.logical_and(ok, here)
        exists.append(ok)
    pxbase = jnp.where(x_first, 0, 16)
    pybase = jnp.where(y_first, -4, 12)
    view = lambda ref: ref.reshape(XR, YP, 128)
    tile = lambda ref: view(ref).at[pl.ds(XO, 32), pl.ds(YO, 32), :]
    pxview = lambda ref: ref.reshape(16, YP, 128).at[:, pl.ds(YO, 32), :]
    pyrows = lambda ref: ref.reshape(XR, PYP, 128).at[pl.ds(XO, 32), pl.ds(4, 16), :]

    loads = [(h_in.at[c], tile(H[c])) for c in range(3)]
    loads += [(e_in.at[c], tile(E[c])) for c in range(3)]
    loads += [(psi_in.at[s], tile(PZ[k])) for k, s in enumerate(Z_SLOTS)]
    loads += [(mat_in, MI)]
    loads = [pltpu.make_async_copy(a, b, in_sem.at[i]) for i, (a, b) in enumerate(loads)]
    for copy in loads:
        copy.start()
    xloads = [
        pltpu.make_async_copy(
            psi_in.at[s, pl.ds(pxbase, 16)], pxview(PX[k]), in_sem.at[12 + k]
        )
        for k, s in enumerate(X_SLOTS)
    ]
    py_local = pl.multiple_of(pybase + 4, 8)
    yloads = [
        pltpu.make_async_copy(
            psi_in.at[s, :, pl.ds(py_local, 16)], pyrows(PY[k]), in_sem.at[16 + k]
        )
        for k, s in enumerate(Y_SLOTS)
    ]

    @pl.when(x_edge)
    def _():
        for copy in xloads:
            copy.start()

    @pl.when(y_edge)
    def _():
        for copy in yloads:
            copy.start()

    barrier = pltpu.get_barrier_semaphore()
    count = 0
    for d, (dx, dy) in enumerate(DIRS):
        count = count + exists[d].astype(jnp.int32)

        @pl.when(exists[d])
        def _(dx=dx, dy=dy):
            pl.semaphore_signal(barrier, inc=1, device_id=(gx + dx, gy + dy), device_id_type=MESH)

    row = lax.broadcasted_iota(jnp.int32, (8, 128), 0)
    lane = lax.broadcasted_iota(jnp.int32, (8, 128), 1)
    zeros = jnp.zeros((8, 128), jnp.float32)
    for half, shift in ((0, 0.5), (1, 0.0)):
        for k, value in enumerate(profile_of(lane.astype(jnp.float32) + shift, 128)):
            ztab[(half * 3 + k) * 8 : (half * 3 + k) * 8 + 8, :] = value
        for i in range(6):
            for tab, offset, extent in (
                (xtab, gx * 32 - XO, nx * 32),
                (ytab, gy * 32 - YO, ny * 32),
            ):
                position = (row + (i * 8 + offset)).astype(jnp.float32) + shift
                for k, value in enumerate(profile_of(position, extent)):
                    at = (half * 3 + k) * 48 + i * 8
                    tab[at : at + 8, :] = value

    def clear(i, c):
        for k in range(4):
            ZB[pl.ds(pl.multiple_of(i * 32 + k * 8, 8), 8), :] = zeros
        return c

    lax.fori_loop(0, 32, clear, 0)
    for ref in E + H:
        for x in (0, 1, 2, 3, 4, 37, 38, 39, 40, 41):
            for k in range(6):
                ref[x * YP + k * 8 : x * YP + k * 8 + 8, :] = zeros

    def clear_rim(i, c):
        base = pl.multiple_of((i + XO) * YP, 8)
        for ref in E + H:
            ref[pl.ds(base, 8), :] = zeros
            ref[pl.ds(base + 40, 8), :] = zeros
        return c

    lax.fori_loop(0, 32, clear_rim, 0)

    zb3 = ZB.reshape(32, 32, 128)
    x_rest = jnp.where(x_first, 16, 0)
    y_rest = pl.multiple_of(jnp.where(y_first, 16, 0), 8)
    zx_all = [pltpu.make_async_copy(zb3, psi_out.at[s], zero_sem.at[k]) for k, s in enumerate(X_SLOTS)]
    zx_half = [
        pltpu.make_async_copy(zb3.at[pl.ds(0, 16)], psi_out.at[s, pl.ds(x_rest, 16)], zero_sem.at[k])
        for k, s in enumerate(X_SLOTS)
    ]
    zy_all = [
        pltpu.make_async_copy(zb3, psi_out.at[s], zero_sem.at[4 + k]) for k, s in enumerate(Y_SLOTS)
    ]
    zy_half = [
        pltpu.make_async_copy(
            zb3.at[:, pl.ds(0, 16)], psi_out.at[s, :, pl.ds(y_rest, 16)], zero_sem.at[4 + k]
        )
        for k, s in enumerate(Y_SLOTS)
    ]

    def zero_fill(act):
        for edge, whole, half in ((x_edge, zx_all, zx_half), (y_edge, zy_all, zy_half)):

            @pl.when(edge)
            def _(half=half):
                for copy in half:
                    act(copy)

            @pl.when(jnp.logical_not(edge))
            def _(whole=whole):
                for copy in whole:
                    act(copy)

    for copy in loads:
        copy.wait()

    @pl.when(x_edge)
    def _():
        for copy in xloads:
            copy.wait()

    @pl.when(y_edge)
    def _():
        for copy in yloads:
            copy.wait()

    zero_fill(lambda copy: copy.start())

    keep_of, drive_of = [], []
    for n in range(NMAT):
        eps = jnp.full((8, 128), eps_in[n], jnp.float32)
        loss = jnp.full((8, 128), sig_in[n], jnp.float32) * time_step / (2.0 * eps)
        keep_of.append((1.0 - loss) / (1.0 + loss))
        drive_of.append((time_step / eps) / (1.0 + loss))

    def choose(bits, table):
        for bit in bits:
            table = [jnp.where(bit, table[i + 1], table[i]) for i in range(0, len(table), 2)]
        return table[0]

    def coefficients(base):
        number = MF[pl.ds(base, 8), :].astype(jnp.int32)
        bits = [(number & (1 << k)) != 0 for k in range(3)]
        KP[pl.ds(base, 8), :] = choose(bits, keep_of)
        DR[pl.ds(base, 8), :] = choose(bits, drive_of)

    at = lambda x, y: (x + XO) * YP + YO + y

    def own_material(x, c):
        for k in range(4):
            MF[pl.ds(at(x, 8 * k), 8), :] = MI[
                pl.ds(pl.multiple_of(x * 32 + 8 * k, 8), 8), :
            ].astype(jnp.float32)
            coefficients(at(x, 8 * k))
        return c

    lax.fori_loop(0, 32, own_material, 0)
    pl.semaphore_wait(barrier, count)

    def remote(d, src, dst, ssem, rsem):
        dx, dy = DIRS[d]
        return pltpu.make_async_remote_copy(
            src_ref=src,
            dst_ref=dst,
            send_sem=ssem,
            recv_sem=rsem,
            device_id=(gx + dx, gy + dy),
            device_id_type=MESH,
        )

    def guarded(d, *copies):
        @pl.when(exists[d])
        def _():
            for copy in copies:
                copy.start()

    def layer_rows(d, layer, q, low):
        if low is None:
            place = layer if DIRS[d][d // 2] < 0 else 31 - layer
        else:
            place = -1 - layer if DIRS[d][d // 2] < 0 else 32 + layer
        if d < 2:
            return pl.ds(at(place, 8 * q) + zero, 8)
        return pl.ds(at(8 * q, place) + zero, 8, stride=YP)

    def pack(parts):
        out = pltpu.roll(parts[3], 112, 1)
        for s in (2, 1, 0):
            out = jnp.where(lane < 32 * (s + 1), pltpu.roll(parts[s], 32 * s + 16, 1), out)
        return out

    def send_face(d, blk):
        buf = send_f[d]

        def one(layer, c):
            for q in range(4):
                rows = layer_rows(d, layer, q, None)
                for k, ref in enumerate(E + H):
                    buf[pl.ds(pl.multiple_of(layer * LAYER + k * 32 + q * 8, 8), 8), :] = ref[
                        rows, :
                    ]
                buf[pl.ds(pl.multiple_of(layer * LAYER + 192 + q * 8, 8), 8), :] = pack(
                    [ref[rows, :] for ref in PZ]
                )
            return c

        lax.fori_loop(0, M, one, 0)
        guarded(d, remote(d, buf, recv_f[OPP[d]].at[blk], s_sem.at[d, 0], r_sem.at[blk, OPP[d], 0]))

    def send_corner(d, blk):
        buf, (dx, dy) = send_c[d - 4], DIRS[d]
        ys = 0 if dy < 0 else 28
        for i in range(M):
            x = i if dx < 0 else 31 - i
            rows = pl.ds(at(x, ys) + zero, 8)
            for k, value in enumerate(
                [ref[rows, :] for ref in E + H] + [pack([ref[rows, :] for ref in PZ])]
            ):
                buf[k * 16 + i * 4 : k * 16 + i * 4 + 4, :] = value[0:4, :]
        copy = remote(
            d, buf, recv_c[OPP[d] - 4].at[blk], s_sem.at[d, 0], r_sem.at[blk, OPP[d], 0]
        )
        guarded(d, copy)

    def edge_rows(d, layer, low):
        if low is None:
            place = layer if DIRS[d][d // 2] < 0 else 31 - layer
        else:
            place = -1 - layer if DIRS[d][d // 2] < 0 else 32 + layer
        if d < 2:
            return [pl.ds((place + XO) * PYP + 4 + 8 * q + zero, 8) for q in range(2)]
        return [pl.ds(8 * q * YP + YO + place + zero, 8, stride=YP) for q in range(2)]

    def send_edge(d, blk):
        @pl.when(jnp.logical_and(exists[d], y_edge if d < 2 else x_edge))
        def _():
            buf = send_e[d]
            for layer in range(M):
                for k, ref in enumerate(PY if d < 2 else PX):
                    for q, rows in enumerate(edge_rows(d, layer, None)):
                        s = layer * 64 + k * 16 + q * 8
                        buf[s : s + 8, :] = ref[rows, :]
            remote(
                d, buf, recv_e[OPP[d]].at[blk], s_sem.at[d, 1], r_sem.at[blk, OPP[d], 1]
            ).start()

    def receive_face(d, blk):
        @pl.when(exists[d])
        def _():
            buf = recv_f[d]
            copy = remote(d, send_f[d], buf.at[blk], s_sem.at[d, 0], r_sem.at[blk, d, 0])
            copy.wait_recv()
            copy.wait_send()

            def unpack(layer, c):
                for q in range(4):
                    rows = layer_rows(d, layer, q, True)
                    for k, ref in enumerate(E + H):
                        ref[rows, :] = buf[
                            blk, pl.ds(pl.multiple_of(layer * LAYER + k * 32 + q * 8, 8), 8), :
                        ]
                    packed = buf[
                        blk, pl.ds(pl.multiple_of(layer * LAYER + 192 + q * 8, 8), 8), :
                    ]
                    for s, ref in enumerate(PZ):
                        ref[rows, :] = pltpu.roll(packed, 112 - 32 * s, 1)
                return c

            lax.fori_loop(0, M, unpack, 0)

    def receive_corner(d, blk):
        @pl.when(exists[d])
        def _():
            buf, (dx, dy) = recv_c[d - 4], DIRS[d]
            copy = remote(d, send_c[d - 4], buf.at[blk], s_sem.at[d, 0], r_sem.at[blk, d, 0])
            copy.wait_recv()
            copy.wait_send()
            ys = -4 if dy < 0 else 32
            for i in range(M):
                x = -1 - i if dx < 0 else 32 + i
                rows = pl.ds(at(x, ys) + zero, 4)
                for k, ref in enumerate(E + H):
                    ref[rows, :] = buf[blk, k * 16 + i * 4 : k * 16 + i * 4 + 4, :]
                packed = buf[blk, 96 + i * 4 : 96 + i * 4 + 4, :]
                for s, ref in enumerate(PZ):
                    ref[rows, :] = pltpu.roll(packed, 112 - 32 * s, 1)

    def receive_edge(d, blk):
        @pl.when(jnp.logical_and(exists[d], y_edge if d < 2 else x_edge))
        def _():
            buf = recv_e[d]
            copy = remote(d, send_e[d], buf.at[blk], s_sem.at[d, 1], r_sem.at[blk, d, 1])
            copy.wait_recv()
            copy.wait_send()
            for layer in range(M):
                for k, ref in enumerate(PY if d < 2 else PX):
                    for q, rows in enumerate(edge_rows(d, layer, True)):
                        s = layer * 64 + k * 16 + q * 8
                        ref[rows, :] = buf[blk, s : s + 8, :]

    for d in range(4):
        for layer in range(M):
            for q in range(4):
                s = layer * 32 + q * 8
                send_m[d][s : s + 8, :] = MF[layer_rows(d, layer, q, None), :]
        guarded(d, remote(d, send_m[d], recv_m[OPP[d]], sm_sem.at[d], rm_sem.at[OPP[d]]))
    for d in range(4, 8):
        dx, dy = DIRS[d]
        for i in range(M):
            rows = pl.ds(at(i if dx < 0 else 31 - i, 0 if dy < 0 else 28) + zero, 4)
            send_mc[d - 4][i * 4 : i * 4 + 4, :] = MF[rows, :]
        guarded(
            d, remote(d, send_mc[d - 4], recv_mc[OPP[d] - 4], sm_sem.at[d], rm_sem.at[OPP[d]])
        )

    def receive_material():
        for x in (0, 1, 2, 3, 4, 37, 38, 39, 40, 41):
            for k in range(6):
                MF[x * YP + k * 8 : x * YP + k * 8 + 8, :] = zeros

        def clear_side(x, c):
            MF[pl.ds(pl.multiple_of((x + XO) * YP, 8), 8), :] = zeros
            MF[pl.ds(pl.multiple_of((x + XO) * YP + 40, 8), 8), :] = zeros
            return c

        lax.fori_loop(0, 32, clear_side, 0)
        for d in range(8):

            @pl.when(exists[d])
            def _(d=d):
                dx, dy = DIRS[d]
                if d < 4:
                    copy = remote(d, send_m[d], recv_m[d], sm_sem.at[d], rm_sem.at[d])
                else:
                    copy = remote(d, send_mc[d - 4], recv_mc[d - 4], sm_sem.at[d], rm_sem.at[d])
                copy.wait_recv()
                copy.wait_send()
                for i in range(M):
                    if d < 4:
                        for q in range(4):
                            s = i * 32 + q * 8
                            MF[layer_rows(d, i, q, True), :] = recv_m[d][s : s + 8, :]
                    else:
                        x = -1 - i if dx < 0 else 32 + i
                        rows = pl.ds(at(x, -4 if dy < 0 else 32) + zero, 4)
                        MF[rows, :] = recv_mc[d - 4][i * 4 : i * 4 + 4, :]

        def whole_row(x, c):
            for k in range(5):
                coefficients(at(x, 8 * k - 4) + zero)
            return c

        def ends_of_row(x, c):
            for k in (0, 4):
                coefficients(at(x, 8 * k - 4) + zero)
            return c

        lax.fori_loop(-4, 0, whole_row, 0)
        lax.fori_loop(32, 36, whole_row, 0)
        lax.fori_loop(0, 32, ends_of_row, 0)

    def table(tab, half, k, start, n):
        return tab[pl.ds(half * 3 * n + k * n + start, 8), :]

    def half_step(half, g, starts, mask_of, px, py):
        source, target = (E, H) if half == 0 else (H, E)
        step = 1 if half == 0 else -1
        zc = [ztab[(half * 3 + k) * 8 : (half * 3 + k) * 8 + 8, :] for k in range(3)]
        keep_lane = lane < 127 if half == 0 else lane > 0
        for r in range(U):
            x = g * U - U + r
            if px:
                xc = [
                    jnp.broadcast_to(xtab[pl.ds((half * 3 + k) * 48 + x + XO, 1), :], (8, 128))
                    for k in range(3)
                ]
            for i, y in enumerate(starts):
                rows = lambda dx, dy: pl.ds(at(x + dx, y + dy) + zero, 8)
                here = rows(0, 0)
                mask = mask_of(r, x, i)

                def put(ref, where, value):
                    pltpu.store(ref.at[where, :], value, mask=mask)

                def diff(a, b):
                    return a - b if half == 0 else b - a

                s0, s1, s2 = (ref[here, :] for ref in source)
                sh = 127 if half == 0 else 1
                turn = lambda v: jnp.where(keep_lane, pltpu.roll(v, sh, 1), 0.0)
                dz1, dz0 = diff(turn(s1), s1), diff(turn(s0), s0)
                dy2 = diff(source[2][rows(0, step), :], s2)
                dy0 = diff(source[0][rows(0, step), :], s0)
                dx2 = diff(source[2][rows(step, 0), :], s2)
                dx1 = diff(source[1][rows(step, 0), :], s1)

                def term(d, coef, ref, where):
                    b, a, q = coef
                    new = b * ref[where, :] + a * d
                    put(ref, where, new)
                    return q * d + new

                tz1 = term(dz1, zc, PZ[2 * half], here)
                tz0 = term(dz0, zc, PZ[2 * half + 1], here)
                if px:
                    there = pl.ds((x - pxbase) * YP + YO + y + zero, 8)
                    tx2 = term(dx2, xc, PX[2 * half], there)
                    tx1 = term(dx1, xc, PX[2 * half + 1], there)
                else:
                    tx2, tx1 = dx2, dx1
                if i in py:
                    yc = [
                        ytab[pl.ds((half * 3 + k) * 48 + YO + y + zero, 8), :] for k in range(3)
                    ]
                    there = pl.ds((x + XO) * PYP + (y - py[i]) + zero, 8)
                    ty2 = term(dy2, yc, PY[2 * half], there)
                    ty0 = term(dy0, yc, PY[2 * half + 1], there)
                else:
                    ty2, ty0 = dy2, dy0
                curls = (ty2 - tz1, tz0 - tx2, tx1 - ty0)
                if half == 0:
                    for ref, c in zip(target, curls):
                        put(ref, here, ref[here, :] - time_step * c)
                else:
                    kp, dr = KP[here, :], DR[here, :]
                    for ref, c in zip(target, curls):
                        put(ref, here, kp * ref[here, :] + dr * c)

    px0 = jnp.where(x_first, 1, jnp.where(x_last, 5, 0))
    px1 = jnp.where(x_first, 5, jnp.where(x_last, 9, 0))

    def groups(half, ga, gb, starts, mask_of, py):
        def plain(part, c):
            first = jnp.where(part == 0, ga, jnp.maximum(ga, px1))
            last = jnp.where(part == 0, jnp.minimum(gb, px0), gb)

            def one(g, c):
                half_step(half, g, starts, mask_of, False, py)
                return c

            return lax.fori_loop(first, last, one, c)

        lax.fori_loop(0, 2, plain, 0)

        def layered(g, c):
            half_step(half, g, starts, mask_of, True, py)
            return c

        lax.fori_loop(jnp.maximum(ga, px0), jnp.minimum(gb, px1), layered, 0)

    def by_place(run, low, high):
        @pl.when(y_first)
        def _():
            run({i: -4 for i in low})

        @pl.when(y_last)
        def _():
            run({i: 12 for i in high})

        @pl.when(jnp.logical_not(y_edge))
        def _():
            run({})

    def inner_range(t, half, first, last):
        lo = jnp.where(first, 0, t - 1 + half)
        hi = jnp.where(last, 32, 32 - t)
        return lo, hi

    def within(v, lo, hi):
        return jnp.logical_and(v >= lo, v < hi)

    starts_a = (0, 8, 16, 24)
    starts_b = (-4, 4, 12, 20, 28)

    def pass_a(t, py):
        for half in range(2):
            xlo, xhi = inner_range(t, half, x_first, x_last)
            ylo, yhi = inner_range(t, half, y_first, y_last)

            def mask_of(r, x, i, xlo=xlo, xhi=xhi, ylo=ylo, yhi=yhi):
                ok = within(x, xlo, xhi).astype(jnp.int32)
                if i in (0, 3):
                    return within(row + starts_a[i], ylo, jnp.where(ok > 0, yhi, -99))
                return row >= 8 - 8 * ok

            groups(half, 1, 9, starts_a, mask_of, py)

    def pass_b(t, py):
        g0 = jnp.where(x_first, 1, 0)
        g1 = jnp.where(x_last, 9, 10)
        ya = jnp.where(y_first, 0, -99)
        yb = jnp.where(y_last, 32, 99)
        for half in range(2):
            xc, xd = inner_range(t, half, x_first, x_last)
            yc, yd = inner_range(t, half, y_first, y_last)

            def mask_of(r, x, i, xc=xc, xd=xd, yc=yc, yd=yd):
                inner = within(x, xc, xd)
                if i not in (0, 4):
                    return row >= 8 * inner.astype(jnp.int32)
                y = row + starts_b[i]
                if i == 0:
                    return within(y, ya, jnp.where(inner, yc, 99))
                return within(y, jnp.where(inner, yd, -99), yb)

            def ends_mask(r, x, i, yc=yc, yd=yd):
                y = row + (-4 if i == 0 else 28)
                return within(y, ya, yc) if i == 0 else within(y, yd, yb)

            def part(p, c, half=half, mask_of=mask_of):
                first = jnp.where(p == 0, g0, 8)
                groups(half, first, jnp.where(p == 0, 2, g1), starts_b, mask_of, py)
                return c

            lax.fori_loop(0, 2, part, 0)
            ends_py = {k // 4: v for k, v in py.items() if k in (0, 4)}
            groups(half, 2, 8, (-4, 28), ends_mask, ends_py)

    def block(turn, c):
        blk = turn % 2
        for d in (0, 1, 2, 3):
            send_face(d, blk)
        for d in range(4, 8):
            send_corner(d, blk)
        for d in range(4):
            send_edge(d, blk)

        def step_a(t, c):
            by_place(lambda py: pass_a(t, py), (0, 1), (2, 3))
            return c

        lax.fori_loop(1, M + 1, step_a, 0)

        @pl.when(turn == 0)
        def _():
            receive_material()

        for d in range(4, 8):
            receive_corner(d, blk)
        for d in range(4):
            receive_edge(d, blk)
        for d in (2, 3, 0, 1):
            receive_face(d, blk)

        def step_b(t, c):
            by_place(lambda py: pass_b(t, py), (0, 1, 2), (2, 3, 4))
            return c

        lax.fori_loop(1, M + 1, step_b, 0)
        return c

    lax.fori_loop(0, STEPS // M, block, 0)

    zero_fill(lambda copy: copy.wait())
    stores = [(tile(E[c]), e_out.at[c]) for c in range(3)]
    stores += [(tile(H[c]), h_out.at[c]) for c in range(3)]
    stores += [(tile(PZ[k]), psi_out.at[s]) for k, s in enumerate(Z_SLOTS)]
    stores = [pltpu.make_async_copy(a, b, out_sem.at[i]) for i, (a, b) in enumerate(stores)]
    xstores = [
        pltpu.make_async_copy(pxview(PX[k]), psi_out.at[s, pl.ds(pxbase, 16)], out_sem.at[12 + k])
        for k, s in enumerate(X_SLOTS)
    ]
    ystores = [
        pltpu.make_async_copy(pyrows(PY[k]), psi_out.at[s, :, pl.ds(py_local, 16)], out_sem.at[16 + k])
        for k, s in enumerate(Y_SLOTS)
    ]

    def finish(act):
        for copy in stores:
            act(copy)

        @pl.when(x_edge)
        def _():
            for copy in xstores:
                act(copy)

        @pl.when(y_edge)
        def _():
            for copy in ystores:
                act(copy)

    finish(lambda copy: copy.start())
    finish(lambda copy: copy.wait())


def solution(mesh):
    nx, ny = mesh.shape["gx"], mesh.shape["gy"]
    f32 = jnp.float32
    field = P(None, "gx", "gy", None)

    def shards(e_field, h_field, psi, material, eps_table, sigma_table):
        big = pltpu.VMEM((XR * YP, 128), f32)
        dma = pltpu.SemaphoreType.DMA
        scratch = [big] * 10
        scratch += [pltpu.VMEM((16 * YP, 128), f32)] * 4
        scratch += [pltpu.VMEM((XR * PYP, 128), f32)] * 4
        scratch += [big, big, big, pltpu.VMEM((1024, 128), jnp.int32), pltpu.VMEM((1024, 128), f32)]
        scratch += [pltpu.VMEM((6 * 48, 128), f32)] * 2 + [pltpu.VMEM((48, 128), f32)]
        scratch += [pltpu.VMEM((FACE, 128), f32)] * 4 + [pltpu.VMEM((2, FACE, 128), f32)] * 4
        scratch += [pltpu.VMEM((CORNER, 128), f32)] * 4 + [pltpu.VMEM((2, CORNER, 128), f32)] * 4
        scratch += [pltpu.VMEM((EDGE, 128), f32)] * 4 + [pltpu.VMEM((2, EDGE, 128), f32)] * 4
        scratch += [pltpu.VMEM((128, 128), f32)] * 8 + [pltpu.VMEM((16, 128), f32)] * 8
        scratch += [
            dma((20,)),
            dma((20,)),
            dma((8,)),
            dma((8, 2)),
            dma((2, 8, 2)),
            dma((8,)),
            dma((8,)),
        ]
        anywhere = pl.BlockSpec(memory_space=pl.ANY)
        smem = pl.BlockSpec(memory_space=pltpu.SMEM)
        return pl.pallas_call(
            functools.partial(kernel, nx, ny),
            out_shape=(
                jax.ShapeDtypeStruct(e_field.shape, f32),
                jax.ShapeDtypeStruct(h_field.shape, f32),
                jax.ShapeDtypeStruct(psi.shape, f32),
            ),
            in_specs=[anywhere] * 4 + [smem] * 2,
            out_specs=(anywhere,) * 3,
            scratch_shapes=scratch,
            compiler_params=pltpu.CompilerParams(collective_id=0, has_side_effects=True),
        )(e_field, h_field, psi, material.reshape(1024, 128), eps_table, sigma_table)

    return jax.shard_map(
        shards,
        mesh=mesh,
        in_specs=(field, field, field, P("gx", "gy", None), P(), P()),
        out_specs=(field, field, field),
        check_vma=False,
    )
```

time: 558 us -> 145 us (0.26)
  the two profiles are of different devices: /device:TPU:96 before, /device:TPU:6 now
where the time goes in v1:
time: 145 us
  Pallas kernels  134 us (92%)
  local copies, waits for them, and re-layouts  10.1 us (7%)
    pallas_call x1, Pallas kernels, shards(): pl.pallas_call(functools.partial(kernel, nx, ny), out_shape=(jax.ShapeDty...  134 us
    unnamed x5, local copies, waits for them, and re-layouts  10.1 us

profile of v1, /device:TPU:6, one launch (start us, length us, event | category | flops | bytes accessed | tf_op | source)
XLA Modules:
  0.0 145.1 jit_solution(1295161544463280946)
XLA Ops:
  0.6 134.3 %shard_map.85 = (f32[3,32,32,128]{3,2,1,0:T(8,128)}, f32[3,32,32,128]{3,2,1,0:T(8,128)}, f32[12,32,32,128]{3,2,1,0:T(8,128)}) custom-call(f32[3,32,32,128]{3,2,1,0:T(8,128)} %e_in.1, f32[3,32,32,128]{3,2,1,0:T(8,128)} %h_in.1, f32[12,32,32,128]{3,2,1,0:T(8,128)} %psi_in.1, s32[1024,128]{1,0:T(8,128)} %bitcast.1, f32[8]{0:T(128)} %eps_in.1, f32[8]{0:T(128)} %sig_in.1), custom_call_target="tpu_custom_call" | custom-call | tf_op jit(solution)/shard_map/pallas_call | solution.py:692
  134.9 0.0 copy-start
  134.9 2.8 %copy.12 = f32[3,32,32,128]{3,2,1,0:T(8,128)} copy(f32[3,32,32,128]{3,2,1,0:T(8,128)} %get-tuple-element.6) | data formatting | bytes 3145728
  137.7 0.0 copy-done
  137.7 1.1 copy.13
  138.9 6.2 %copy.14 = f32[12,32,32,128]{3,2,1,0:T(8,128)} copy(f32[12,32,32,128]{3,2,1,0:T(8,128)} %get-tuple-element.8) | data formatting | bytes 12582912
Async XLA Ops:
  134.9 2.8 %copy-start = (f32[3,32,32,128]{3,2,1,0:T(8,128)S(1)}, f32[3,32,32,128]{3,2,1,0:T(8,128)}, u32[]{:S(2)}) copy-start(f32[3,32,32,128]{3,2,1,0:T(8,128)} %get-tuple-element.7) | copy-start | bytes 4718596

commit v2 on v1

--- a/solution.py
+++ b/solution.py
@@ -16,6 +16,8 @@
 alpha_peak = 0.05
 
 M = 4
+D = 2
+PXR = 24
 XO, XR = 5, 42
 YO, YP = 8, 48
 PYP = 24
@@ -28,9 +30,12 @@
 DIRS = ((-1, 0), (1, 0), (0, -1), (0, 1), (-1, -1), (-1, 1), (1, -1), (1, 1))
 OPP = (1, 0, 3, 2, 7, 6, 5, 4)
 LAYER = NA * 32
-FACE = M * LAYER
-CORNER = NA * M * M
-EDGE = M * 4 * 16
+ENDS = D * LAYER
+EXTRA = ENDS + 2 * NA * 4
+FACE = EXTRA + 64
+CORNER_ROWS = ((0, 4), (4, 3), (7, 2), (9, 1))
+CORNER = NA * 10
+EDGE = D * 4 * 16
 
 
 def profile_of(position, extent):
@@ -48,23 +53,90 @@
     return jnp.where(inside, b, 0.0), jnp.where(inside, a, 0.0), 1.0 / kappa
 
 
-def kernel(nx, ny, e_in, h_in, psi_in, mat_in, eps_in, sig_in, e_out, h_out, psi_out, *scratch):
+def views(nx, ny):
+    gx, gy = lax.axis_index("gx"), lax.axis_index("gy")
+    x_first, x_last = gx == 0, gx == nx - 1
+    y_first, y_last = gy == 0, gy == ny - 1
+    tile = lambda ref: ref.reshape(XR, YP, 128).at[pl.ds(XO, 32), pl.ds(YO, 32), :]
+    pxview = lambda ref: ref.reshape(PXR, YP, 128).at[pl.ds(4, 16), pl.ds(YO, 32), :]
+    pyrows = lambda ref: ref.reshape(XR, PYP, 128).at[pl.ds(XO, 32), pl.ds(4, 16), :]
+    x_layer = jnp.where(x_first, 0, 16)
+    y_layer = pl.multiple_of(jnp.where(y_first, 0, 16), 8)
+    return x_first, x_last, y_first, y_last, tile, pxview, pyrows, x_layer, y_layer
+
+
+def store_kernel(nx, ny, *refs):
+    refs = list(refs)
+    take = lambda n: [refs.pop(0) for _ in range(n)]
+    E, H, PZ, PX, PY = take(3), take(3), take(4), take(4), take(4)
+    e_out, h_out, psi_out, ZB, sem, edge_sem = refs
+    x_first, x_last, y_first, y_last, tile, pxview, pyrows, x_layer, y_layer = views(nx, ny)
+    start = lambda copy: copy.start()
+    wait = lambda copy: copy.wait()
+    stores = [(tile(E[c]), e_out.at[c]) for c in range(3)]
+    stores += [(tile(H[c]), h_out.at[c]) for c in range(3)]
+    stores += [(tile(PZ[k]), psi_out.at[s]) for k, s in enumerate(Z_SLOTS)]
+    stores = [pltpu.make_async_copy(a, b, sem.at[i]) for i, (a, b) in enumerate(stores)]
+    for copy in stores:
+        copy.start()
+
+    def clear(i, c):
+        for k in range(8):
+            ZB[pl.ds(pl.multiple_of(i * 64 + k * 8, 8), 8), :] = jnp.zeros((8, 128), jnp.float32)
+        return c
+
+    lax.fori_loop(0, 16, clear, 0)
+    zb = ZB.reshape(32, 32, 128)
+    x_rest = 16 - x_layer
+    y_rest = pl.multiple_of(16 - y_layer, 8)
+
+    def rest(act):
+        for edge, slots, refs, first in (
+            (jnp.logical_or(x_first, x_last), X_SLOTS, PX, 0),
+            (jnp.logical_or(y_first, y_last), Y_SLOTS, PY, 4),
+        ):
+
+            @pl.when(edge)
+            def _(slots=slots, refs=refs, first=first):
+                for k, s in enumerate(slots):
+                    if first == 0:
+                        out = psi_out.at[s, pl.ds(x_layer, 16)]
+                        other = psi_out.at[s, pl.ds(x_rest, 16)]
+                        kept, none = pxview(refs[k]), zb.at[pl.ds(0, 16)]
+                    else:
+                        out = psi_out.at[s, :, pl.ds(y_layer, 16)]
+                        other = psi_out.at[s, :, pl.ds(y_rest, 16)]
+                        kept, none = pyrows(refs[k]), zb.at[:, pl.ds(0, 16)]
+                    act(pltpu.make_async_copy(kept, out, edge_sem.at[0, first + k]))
+                    act(pltpu.make_async_copy(none, other, edge_sem.at[1, first + k]))
+
+            @pl.when(jnp.logical_not(edge))
+            def _(slots=slots, first=first):
+                for k, s in enumerate(slots):
+                    act(pltpu.make_async_copy(zb, psi_out.at[s], edge_sem.at[0, first + k]))
+
+    rest(start)
+    rest(wait)
+    for copy in stores:
+        copy.wait()
+
+
+def kernel(nx, ny, e_in, h_in, psi_in, mat_in, eps_in, sig_in, *scratch):
     scratch = list(scratch)
     take = lambda n: [scratch.pop(0) for _ in range(n)]
     E, H, PZ, PX, PY = take(3), take(3), take(4), take(4), take(4)
-    KP, DR, MF, MI, ZB = take(5)
+    KP, DR, MF, MI = take(4)
     xtab, ytab, ztab = take(1)[0], take(1)[0], take(1)[0]
     send_f, recv_f = take(4), take(4)
     send_c, recv_c = take(4), take(4)
     send_e, recv_e = take(4), take(4)
     send_m, recv_m = take(4), take(4)
     send_mc, recv_mc = take(4), take(4)
-    in_sem, out_sem, zero_sem, s_sem, r_sem, sm_sem, rm_sem = take(7)
+    in_sem, s_sem, r_sem, sm_sem, rm_sem = take(5)
 
     gx, gy = lax.axis_index("gx"), lax.axis_index("gy")
     zero = jnp.minimum(gx, 0)
-    x_first, x_last = gx == 0, gx == nx - 1
-    y_first, y_last = gy == 0, gy == ny - 1
+    x_first, x_last, y_first, y_last, tile, pxview, pyrows, x_layer, y_layer = views(nx, ny)
     x_edge = jnp.logical_or(x_first, x_last)
     y_edge = jnp.logical_or(y_first, y_last)
     exists = []
@@ -77,10 +149,6 @@
         exists.append(ok)
     pxbase = jnp.where(x_first, 0, 16)
     pybase = jnp.where(y_first, -4, 12)
-    view = lambda ref: ref.reshape(XR, YP, 128)
-    tile = lambda ref: view(ref).at[pl.ds(XO, 32), pl.ds(YO, 32), :]
-    pxview = lambda ref: ref.reshape(16, YP, 128).at[:, pl.ds(YO, 32), :]
-    pyrows = lambda ref: ref.reshape(XR, PYP, 128).at[pl.ds(XO, 32), pl.ds(4, 16), :]
 
     loads = [(h_in.at[c], tile(H[c])) for c in range(3)]
     loads += [(e_in.at[c], tile(E[c])) for c in range(3)]
@@ -91,14 +159,13 @@
         copy.start()
     xloads = [
         pltpu.make_async_copy(
-            psi_in.at[s, pl.ds(pxbase, 16)], pxview(PX[k]), in_sem.at[12 + k]
+            psi_in.at[s, pl.ds(x_layer, 16)], pxview(PX[k]), in_sem.at[12 + k]
         )
         for k, s in enumerate(X_SLOTS)
     ]
-    py_local = pl.multiple_of(pybase + 4, 8)
     yloads = [
         pltpu.make_async_copy(
-            psi_in.at[s, :, pl.ds(py_local, 16)], pyrows(PY[k]), in_sem.at[16 + k]
+            psi_in.at[s, :, pl.ds(y_layer, 16)], pyrows(PY[k]), in_sem.at[16 + k]
         )
         for k, s in enumerate(Y_SLOTS)
     ]
@@ -138,12 +205,6 @@
                     at = (half * 3 + k) * 48 + i * 8
                     tab[at : at + 8, :] = value
 
-    def clear(i, c):
-        for k in range(4):
-            ZB[pl.ds(pl.multiple_of(i * 32 + k * 8, 8), 8), :] = zeros
-        return c
-
-    lax.fori_loop(0, 32, clear, 0)
     for ref in E + H:
         for x in (0, 1, 2, 3, 4, 37, 38, 39, 40, 41):
             for k in range(6):
@@ -158,36 +219,13 @@
 
     lax.fori_loop(0, 32, clear_rim, 0)
 
-    zb3 = ZB.reshape(32, 32, 128)
-    x_rest = jnp.where(x_first, 16, 0)
-    y_rest = pl.multiple_of(jnp.where(y_first, 16, 0), 8)
-    zx_all = [pltpu.make_async_copy(zb3, psi_out.at[s], zero_sem.at[k]) for k, s in enumerate(X_SLOTS)]
-    zx_half = [
-        pltpu.make_async_copy(zb3.at[pl.ds(0, 16)], psi_out.at[s, pl.ds(x_rest, 16)], zero_sem.at[k])
-        for k, s in enumerate(X_SLOTS)
-    ]
-    zy_all = [
-        pltpu.make_async_copy(zb3, psi_out.at[s], zero_sem.at[4 + k]) for k, s in enumerate(Y_SLOTS)
-    ]
-    zy_half = [
-        pltpu.make_async_copy(
-            zb3.at[:, pl.ds(0, 16)], psi_out.at[s, :, pl.ds(y_rest, 16)], zero_sem.at[4 + k]
-        )
-        for k, s in enumerate(Y_SLOTS)
-    ]
-
-    def zero_fill(act):
-        for edge, whole, half in ((x_edge, zx_all, zx_half), (y_edge, zy_all, zy_half)):
-
-            @pl.when(edge)
-            def _(half=half):
-                for copy in half:
-                    act(copy)
-
-            @pl.when(jnp.logical_not(edge))
-            def _(whole=whole):
-                for copy in whole:
-                    act(copy)
+    def clear_beside(i, c):
+        for ref in PX:
+            for start in (0, 20 * YP):
+                ref[pl.ds(pl.multiple_of(start + i * 8, 8), 8), :] = zeros
+        return c
+
+    lax.fori_loop(0, 4 * YP // 8, clear_beside, 0)
 
     for copy in loads:
         copy.wait()
@@ -201,8 +239,6 @@
     def _():
         for copy in yloads:
             copy.wait()
-
-    zero_fill(lambda copy: copy.start())
 
     keep_of, drive_of = [], []
     for n in range(NMAT):
@@ -262,39 +298,68 @@
         return pl.ds(at(8 * q, place) + zero, 8, stride=YP)
 
     def pack(parts):
+        lanes = lax.broadcasted_iota(jnp.int32, parts[0].shape, 1)
         out = pltpu.roll(parts[3], 112, 1)
         for s in (2, 1, 0):
-            out = jnp.where(lane < 32 * (s + 1), pltpu.roll(parts[s], 32 * s + 16, 1), out)
+            out = jnp.where(lanes < 32 * (s + 1), pltpu.roll(parts[s], 32 * s + 16, 1), out)
         return out
 
-    def send_face(d, blk):
+    def gather(rows):
+        return [ref[rows, :] for ref in E + H] + [pack([ref[rows, :] for ref in PZ])]
+
+    def scatter(rows, values):
+        for ref, value in zip(E + H, values):
+            ref[rows, :] = value
+        for s, ref in enumerate(PZ):
+            ref[rows, :] = pltpu.roll(values[6], 112 - 32 * s, 1)
+
+    def end_rows(d, layer, end, low):
+        if low is None:
+            place = layer if DIRS[d][d // 2] < 0 else 31 - layer
+        else:
+            place = -1 - layer if DIRS[d][d // 2] < 0 else 32 + layer
+        if d < 2:
+            return pl.ds(at(place, 30 * end) + zero, 2)
+        return pl.ds(at(30 * end, place) + zero, 2, stride=YP)
+
+    def face_copy(d, blk, start, n, k, incoming):
+        span = pl.ds(start, n)
+        to = d if incoming else OPP[d]
+        return remote(
+            d, send_f[d].at[span], recv_f[to].at[blk, span], s_sem.at[d, k], r_sem.at[blk, to, k]
+        )
+
+    def send_layer(d, layer, blk):
         buf = send_f[d]
-
-        def one(layer, c):
-            for q in range(4):
-                rows = layer_rows(d, layer, q, None)
-                for k, ref in enumerate(E + H):
-                    buf[pl.ds(pl.multiple_of(layer * LAYER + k * 32 + q * 8, 8), 8), :] = ref[
-                        rows, :
-                    ]
-                buf[pl.ds(pl.multiple_of(layer * LAYER + 192 + q * 8, 8), 8), :] = pack(
-                    [ref[rows, :] for ref in PZ]
-                )
-            return c
-
-        lax.fori_loop(0, M, one, 0)
-        guarded(d, remote(d, buf, recv_f[OPP[d]].at[blk], s_sem.at[d, 0], r_sem.at[blk, OPP[d], 0]))
+        for q in range(4):
+            for k, value in enumerate(gather(layer_rows(d, layer, q, None))):
+                buf[pl.ds(pl.multiple_of(layer * LAYER + k * 32 + q * 8, 8), 8), :] = value
+        guarded(d, face_copy(d, blk, pl.multiple_of(layer * LAYER, 8), LAYER, layer, False))
+
+    extra_fields = {1: (H[1], H[2]), 3: (H[2], H[0])}
+    tail_rows = lambda d: (FACE if d in (1, 3) else EXTRA) - ENDS
+
+    def send_tail(d, blk):
+        buf = send_f[d]
+        for layer in range(2):
+            for end in range(2):
+                for k, value in enumerate(gather(end_rows(d, D + layer, end, None))):
+                    s = ENDS + layer * NA * 4 + k * 4 + end * 2
+                    buf[s : s + 2, :] = value
+        if d in extra_fields:
+            for k, ref in enumerate(extra_fields[d]):
+                for q in range(4):
+                    s = EXTRA + k * 32 + q * 8
+                    buf[s : s + 8, :] = ref[layer_rows(d, D, q, None), :]
+        guarded(d, face_copy(d, blk, ENDS, tail_rows(d), D, False))
 
     def send_corner(d, blk):
         buf, (dx, dy) = send_c[d - 4], DIRS[d]
-        ys = 0 if dy < 0 else 28
-        for i in range(M):
+        for i, (first, n) in enumerate(CORNER_ROWS):
             x = i if dx < 0 else 31 - i
-            rows = pl.ds(at(x, ys) + zero, 8)
-            for k, value in enumerate(
-                [ref[rows, :] for ref in E + H] + [pack([ref[rows, :] for ref in PZ])]
-            ):
-                buf[k * 16 + i * 4 : k * 16 + i * 4 + 4, :] = value[0:4, :]
+            rows = pl.ds(at(x, 0 if dy < 0 else 32 - n) + zero, n)
+            for k, value in enumerate(gather(rows)):
+                buf[k * 10 + first : k * 10 + first + n, :] = value
         copy = remote(
             d, buf, recv_c[OPP[d] - 4].at[blk], s_sem.at[d, 0], r_sem.at[blk, OPP[d], 0]
         )
@@ -307,44 +372,56 @@
             place = -1 - layer if DIRS[d][d // 2] < 0 else 32 + layer
         if d < 2:
             return [pl.ds((place + XO) * PYP + 4 + 8 * q + zero, 8) for q in range(2)]
-        return [pl.ds(8 * q * YP + YO + place + zero, 8, stride=YP) for q in range(2)]
+        return [pl.ds((8 * q + 4) * YP + YO + place + zero, 8, stride=YP) for q in range(2)]
 
     def send_edge(d, blk):
         @pl.when(jnp.logical_and(exists[d], y_edge if d < 2 else x_edge))
         def _():
             buf = send_e[d]
-            for layer in range(M):
+            for layer in range(D):
                 for k, ref in enumerate(PY if d < 2 else PX):
                     for q, rows in enumerate(edge_rows(d, layer, None)):
                         s = layer * 64 + k * 16 + q * 8
                         buf[s : s + 8, :] = ref[rows, :]
             remote(
-                d, buf, recv_e[OPP[d]].at[blk], s_sem.at[d, 1], r_sem.at[blk, OPP[d], 1]
+                d, buf, recv_e[OPP[d]].at[blk], s_sem.at[d, D + 1], r_sem.at[blk, OPP[d], D + 1]
             ).start()
 
     def receive_face(d, blk):
         @pl.when(exists[d])
         def _():
             buf = recv_f[d]
-            copy = remote(d, send_f[d], buf.at[blk], s_sem.at[d, 0], r_sem.at[blk, d, 0])
-            copy.wait_recv()
-            copy.wait_send()
+            for k in range(D + 1):
+                start, size = (k * LAYER, LAYER) if k < D else (ENDS, tail_rows(d))
+                face_copy(d, blk, start, size, k, True).wait_send()
+                if k == D:
+                    size = tail_rows(OPP[d])
+                face_copy(d, blk, start, size, k, True).wait_recv()
 
             def unpack(layer, c):
                 for q in range(4):
-                    rows = layer_rows(d, layer, q, True)
-                    for k, ref in enumerate(E + H):
-                        ref[rows, :] = buf[
-                            blk, pl.ds(pl.multiple_of(layer * LAYER + k * 32 + q * 8, 8), 8), :
-                        ]
-                    packed = buf[
-                        blk, pl.ds(pl.multiple_of(layer * LAYER + 192 + q * 8, 8), 8), :
-                    ]
-                    for s, ref in enumerate(PZ):
-                        ref[rows, :] = pltpu.roll(packed, 112 - 32 * s, 1)
+                    scatter(
+                        layer_rows(d, layer, q, True),
+                        [
+                            buf[blk, pl.ds(pl.multiple_of(layer * LAYER + k * 32 + q * 8, 8), 8), :]
+                            for k in range(NA)
+                        ],
+                    )
                 return c
 
-            lax.fori_loop(0, M, unpack, 0)
+            lax.fori_loop(0, D, unpack, 0)
+            for layer in range(2):
+                for end in range(2):
+                    s = ENDS + layer * NA * 4 + end * 2
+                    scatter(
+                        end_rows(d, D + layer, end, True),
+                        [buf[blk, s + 4 * k : s + 4 * k + 2, :] for k in range(NA)],
+                    )
+            if OPP[d] in extra_fields:
+                for k, ref in enumerate(extra_fields[OPP[d]]):
+                    for q in range(4):
+                        s = EXTRA + k * 32 + q * 8
+                        ref[layer_rows(d, D, q, True), :] = buf[blk, s : s + 8, :]
 
     def receive_corner(d, blk):
         @pl.when(exists[d])
@@ -353,24 +430,22 @@
             copy = remote(d, send_c[d - 4], buf.at[blk], s_sem.at[d, 0], r_sem.at[blk, d, 0])
             copy.wait_recv()
             copy.wait_send()
-            ys = -4 if dy < 0 else 32
-            for i in range(M):
+            for i, (first, n) in enumerate(CORNER_ROWS):
                 x = -1 - i if dx < 0 else 32 + i
-                rows = pl.ds(at(x, ys) + zero, 4)
-                for k, ref in enumerate(E + H):
-                    ref[rows, :] = buf[blk, k * 16 + i * 4 : k * 16 + i * 4 + 4, :]
-                packed = buf[blk, 96 + i * 4 : 96 + i * 4 + 4, :]
-                for s, ref in enumerate(PZ):
-                    ref[rows, :] = pltpu.roll(packed, 112 - 32 * s, 1)
+                s = lambda k: k * 10 + first
+                scatter(
+                    pl.ds(at(x, -n if dy < 0 else 32) + zero, n),
+                    [buf[blk, s(k) : s(k) + n, :] for k in range(NA)],
+                )
 
     def receive_edge(d, blk):
         @pl.when(jnp.logical_and(exists[d], y_edge if d < 2 else x_edge))
         def _():
             buf = recv_e[d]
-            copy = remote(d, send_e[d], buf.at[blk], s_sem.at[d, 1], r_sem.at[blk, d, 1])
+            copy = remote(d, send_e[d], buf.at[blk], s_sem.at[d, D + 1], r_sem.at[blk, d, D + 1])
             copy.wait_recv()
             copy.wait_send()
-            for layer in range(M):
+            for layer in range(D):
                 for k, ref in enumerate(PY if d < 2 else PX):
                     for q, rows in enumerate(edge_rows(d, layer, True)):
                         s = layer * 64 + k * 16 + q * 8
@@ -440,13 +515,13 @@
     def table(tab, half, k, start, n):
         return tab[pl.ds(half * 3 * n + k * n + start, 8), :]
 
-    def half_step(half, g, starts, mask_of, px, py):
+    def half_step(half, x0, starts, mask_of, px, py):
         source, target = (E, H) if half == 0 else (H, E)
         step = 1 if half == 0 else -1
         zc = [ztab[(half * 3 + k) * 8 : (half * 3 + k) * 8 + 8, :] for k in range(3)]
         keep_lane = lane < 127 if half == 0 else lane > 0
         for r in range(U):
-            x = g * U - U + r
+            x = x0 + r
             if px:
                 xc = [
                     jnp.broadcast_to(xtab[pl.ds((half * 3 + k) * 48 + x + XO, 1), :], (8, 128))
@@ -481,7 +556,7 @@
                 tz1 = term(dz1, zc, PZ[2 * half], here)
                 tz0 = term(dz0, zc, PZ[2 * half + 1], here)
                 if px:
-                    there = pl.ds((x - pxbase) * YP + YO + y + zero, 8)
+                    there = pl.ds((x - pxbase + 4) * YP + YO + y + zero, 8)
                     tx2 = term(dx2, xc, PX[2 * half], there)
                     tx1 = term(dx1, xc, PX[2 * half + 1], there)
                 else:
@@ -504,27 +579,28 @@
                     for ref, c in zip(target, curls):
                         put(ref, here, kp * ref[here, :] + dr * c)
 
-    px0 = jnp.where(x_first, 1, jnp.where(x_last, 5, 0))
-    px1 = jnp.where(x_first, 5, jnp.where(x_last, 9, 0))
-
-    def groups(half, ga, gb, starts, mask_of, py):
+    px0 = jnp.where(x_first, 0, jnp.where(x_last, 16, -32))
+    px1 = jnp.where(x_edge, px0 + 16, -32)
+
+    def groups(half, xs, xe, starts, mask_of, py):
+        n = (xe - xs + U - 1) // U
+        ia = jnp.clip((px0 - xs + 64) // U - 64 // U, 0, n)
+        ib = jnp.clip((px1 - xs + 64 + U - 1) // U - 64 // U, 0, n)
+
         def plain(part, c):
-            first = jnp.where(part == 0, ga, jnp.maximum(ga, px1))
-            last = jnp.where(part == 0, jnp.minimum(gb, px0), gb)
-
-            def one(g, c):
-                half_step(half, g, starts, mask_of, False, py)
+            def one(i, c):
+                half_step(half, xs + U * i, starts, mask_of, False, py)
                 return c
 
-            return lax.fori_loop(first, last, one, c)
+            return lax.fori_loop(jnp.where(part == 0, 0, ib), jnp.where(part == 0, ia, n), one, c)
 
         lax.fori_loop(0, 2, plain, 0)
 
-        def layered(g, c):
-            half_step(half, g, starts, mask_of, True, py)
+        def layered(i, c):
+            half_step(half, xs + U * i, starts, mask_of, True, py)
             return c
 
-        lax.fori_loop(jnp.maximum(ga, px0), jnp.minimum(gb, px1), layered, 0)
+        lax.fori_loop(ia, ib, layered, 0)
 
     def by_place(run, low, high):
         @pl.when(y_first)
@@ -561,50 +637,82 @@
                     return within(row + starts_a[i], ylo, jnp.where(ok > 0, yhi, -99))
                 return row >= 8 - 8 * ok
 
-            groups(half, 1, 9, starts_a, mask_of, py)
+            groups(half, xlo, xhi, starts_a, mask_of, py)
 
     def pass_b(t, py):
-        g0 = jnp.where(x_first, 1, 0)
-        g1 = jnp.where(x_last, 9, 10)
         ya = jnp.where(y_first, 0, -99)
         yb = jnp.where(y_last, 32, 99)
         for half in range(2):
             xc, xd = inner_range(t, half, x_first, x_last)
             yc, yd = inner_range(t, half, y_first, y_last)
-
-            def mask_of(r, x, i, xc=xc, xd=xd, yc=yc, yd=yd):
-                inner = within(x, xc, xd)
+            grow = t - 1 + half
+            xa = jnp.where(x_first, 0, -t)
+            xb = jnp.where(x_last, 32, 32 + grow)
+            wa = jnp.where(y_first, 0, -t)
+            wb = jnp.where(y_last, 32, 32 + grow)
+            low = jnp.maximum(-t, t - 5 + half)
+            high = 32 - t
+            xs = jnp.where(x_first, 0, low + U)
+            xe = jnp.where(x_last, 32, high)
+
+            def mask_of(r, x, i, xa=xa, xb=xb, xc=xc, xd=xd, yc=yc, yd=yd, wa=wa, wb=wb):
+                border = jnp.logical_or(within(x, xa, xc), within(x, xd, xb))
                 if i not in (0, 4):
-                    return row >= 8 * inner.astype(jnp.int32)
+                    return row >= 8 - 8 * border.astype(jnp.int32)
                 y = row + starts_b[i]
                 if i == 0:
-                    return within(y, ya, jnp.where(inner, yc, 99))
-                return within(y, jnp.where(inner, yd, -99), yb)
-
-            def ends_mask(r, x, i, yc=yc, yd=yd):
+                    return within(y, jnp.where(border, ya, wa), jnp.where(border, 99, yc))
+                return within(y, jnp.where(border, -99, yd), jnp.where(border, yb, wb))
+
+            def ends_mask(r, x, i, yc=yc, yd=yd, wa=wa, wb=wb, xe=xe):
                 y = row + (-4 if i == 0 else 28)
-                return within(y, ya, yc) if i == 0 else within(y, yd, yb)
-
-            def part(p, c, half=half, mask_of=mask_of):
-                first = jnp.where(p == 0, g0, 8)
-                groups(half, first, jnp.where(p == 0, 2, g1), starts_b, mask_of, py)
+                if i == 0:
+                    return within(y, wa, jnp.where(x < xe, yc, -99))
+                return within(y, yd, jnp.where(x < xe, wb, -99))
+
+            def border(p, c, half=half, low=low, high=high, mask_of=mask_of):
+                half_step(half, jnp.where(p == 0, low, high), starts_b, mask_of, False, py)
                 return c
 
-            lax.fori_loop(0, 2, part, 0)
+            lax.fori_loop(jnp.where(x_first, 1, 0), jnp.where(x_last, 1, 2), border, 0)
             ends_py = {k // 4: v for k, v in py.items() if k in (0, 4)}
-            groups(half, 2, 8, (-4, 28), ends_mask, ends_py)
+            groups(half, xs, xe, (-4, 28), ends_mask, ends_py)
+
+            def outside_mask(r, x, i, low=low, yc=yc, yd=yd, wa=wa, wb=wb):
+                y = row + (-4 if i == 0 else 28)
+                if i == 0:
+                    return within(y, wa, jnp.where(x < low, yc, -99))
+                return within(y, yd, jnp.where(x < low, wb, -99))
+
+            @pl.when(jnp.logical_and(jnp.logical_not(x_first), low + 5 - t - half > 0))
+            def _(half=half, outside_mask=outside_mask):
+                half_step(half, t - 5 + half, (-4, 28), outside_mask, False, ends_py)
 
     def block(turn, c):
         blk = turn % 2
-        for d in (0, 1, 2, 3):
-            send_face(d, blk)
-        for d in range(4, 8):
-            send_corner(d, blk)
-        for d in range(4):
-            send_edge(d, blk)
 
         def step_a(t, c):
+            @pl.when(t <= D)
+            def _():
+                send_layer(1, t - 1, blk)
+                send_layer(3, t - 1, blk)
+
             by_place(lambda py: pass_a(t, py), (0, 1), (2, 3))
+
+            @pl.when(t <= D)
+            def _():
+                send_layer(0, t - 1, blk)
+                send_layer(2, t - 1, blk)
+
+            @pl.when(t == D)
+            def _():
+                for d in range(4):
+                    send_tail(d, blk)
+                for d in range(4, 8):
+                    send_corner(d, blk)
+                for d in range(4):
+                    send_edge(d, blk)
+
             return c
 
         lax.fori_loop(1, M + 1, step_a, 0)
@@ -629,37 +737,6 @@
 
     lax.fori_loop(0, STEPS // M, block, 0)
 
-    zero_fill(lambda copy: copy.wait())
-    stores = [(tile(E[c]), e_out.at[c]) for c in range(3)]
-    stores += [(tile(H[c]), h_out.at[c]) for c in range(3)]
-    stores += [(tile(PZ[k]), psi_out.at[s]) for k, s in enumerate(Z_SLOTS)]
-    stores = [pltpu.make_async_copy(a, b, out_sem.at[i]) for i, (a, b) in enumerate(stores)]
-    xstores = [
-        pltpu.make_async_copy(pxview(PX[k]), psi_out.at[s, pl.ds(pxbase, 16)], out_sem.at[12 + k])
-        for k, s in enumerate(X_SLOTS)
-    ]
-    ystores = [
-        pltpu.make_async_copy(pyrows(PY[k]), psi_out.at[s, :, pl.ds(py_local, 16)], out_sem.at[16 + k])
-        for k, s in enumerate(Y_SLOTS)
-    ]
-
-    def finish(act):
-        for copy in stores:
-            act(copy)
-
-        @pl.when(x_edge)
-        def _():
-            for copy in xstores:
-                act(copy)
-
-        @pl.when(y_edge)
-        def _():
-            for copy in ystores:
-                act(copy)
-
-    finish(lambda copy: copy.start())
-    finish(lambda copy: copy.wait())
-
 
 def solution(mesh):
     nx, ny = mesh.shape["gx"], mesh.shape["gy"]
@@ -669,10 +746,8 @@
     def shards(e_field, h_field, psi, material, eps_table, sigma_table):
         big = pltpu.VMEM((XR * YP, 128), f32)
         dma = pltpu.SemaphoreType.DMA
-        scratch = [big] * 10
-        scratch += [pltpu.VMEM((16 * YP, 128), f32)] * 4
-        scratch += [pltpu.VMEM((XR * PYP, 128), f32)] * 4
-        scratch += [big, big, big, pltpu.VMEM((1024, 128), jnp.int32), pltpu.VMEM((1024, 128), f32)]
+        kept = [(XR * YP, 128)] * 10 + [(PXR * YP, 128)] * 4 + [(XR * PYP, 128)] * 4
+        scratch = [big, big, big, pltpu.VMEM((1024, 128), jnp.int32)]
         scratch += [pltpu.VMEM((6 * 48, 128), f32)] * 2 + [pltpu.VMEM((48, 128), f32)]
         scratch += [pltpu.VMEM((FACE, 128), f32)] * 4 + [pltpu.VMEM((2, FACE, 128), f32)] * 4
         scratch += [pltpu.VMEM((CORNER, 128), f32)] * 4 + [pltpu.VMEM((2, CORNER, 128), f32)] * 4
@@ -680,27 +755,33 @@
         scratch += [pltpu.VMEM((128, 128), f32)] * 8 + [pltpu.VMEM((16, 128), f32)] * 8
         scratch += [
             dma((20,)),
-            dma((20,)),
-            dma((8,)),
-            dma((8, 2)),
-            dma((2, 8, 2)),
+            dma((8, D + 2)),
+            dma((2, 8, D + 2)),
             dma((8,)),
             dma((8,)),
         ]
         anywhere = pl.BlockSpec(memory_space=pl.ANY)
         smem = pl.BlockSpec(memory_space=pltpu.SMEM)
+        vmem = pl.BlockSpec(memory_space=pltpu.VMEM)
+        state = pl.pallas_call(
+            functools.partial(kernel, nx, ny),
+            out_shape=[pltpu.VMEM(shape, f32) for shape in kept],
+            in_specs=[anywhere] * 4 + [smem] * 2,
+            out_specs=[vmem] * len(kept),
+            scratch_shapes=scratch,
+            compiler_params=pltpu.CompilerParams(
+                collective_id=0, has_side_effects=True, vmem_limit_bytes=40 << 20
+            ),
+        )(e_field, h_field, psi, material.reshape(1024, 128), eps_table, sigma_table)
+        state = [pltpu.with_memory_space_constraint(a, pltpu.VMEM) for a in state]
         return pl.pallas_call(
-            functools.partial(kernel, nx, ny),
-            out_shape=(
-                jax.ShapeDtypeStruct(e_field.shape, f32),
-                jax.ShapeDtypeStruct(h_field.shape, f32),
-                jax.ShapeDtypeStruct(psi.shape, f32),
-            ),
-            in_specs=[anywhere] * 4 + [smem] * 2,
-            out_specs=(anywhere,) * 3,
-            scratch_shapes=scratch,
-            compiler_params=pltpu.CompilerParams(collective_id=0, has_side_effects=True),
-        )(e_field, h_field, psi, material.reshape(1024, 128), eps_table, sigma_table)
+            functools.partial(store_kernel, nx, ny),
+            out_shape=[jax.ShapeDtypeStruct(a.shape, f32) for a in (e_field, h_field, psi)],
+            in_specs=[vmem] * len(kept),
+            out_specs=[anywhere] * 3,
+            scratch_shapes=[pltpu.VMEM((1024, 128), f32), dma((10,)), dma((2, 8))],
+            compiler_params=pltpu.CompilerParams(vmem_limit_bytes=8 << 20),
+        )(*state)
 
     return jax.shard_map(
         shards,

time: 145 us -> 108 us (0.74)
  Pallas kernels: 134 us -> 108 us
  local copies, waits for them, and re-layouts: 10.1 us -> 0 us
    pallas_call x1 -> x2, Pallas kernels: 134 us -> 108 us  [the longest x1 104 us: shards(): pl.pallas_call(functools.partial(kernel, nx, ny), out_shape=[pltpu.VMEM(s...]
    unnamed x5 -> x0, local copies, waits for them, and re-layouts: 10.1 us -> none
where the time goes in v2:
time: 108 us
  Pallas kernels  108 us (100%)
    pallas_call x1, Pallas kernels, shards(): pl.pallas_call(functools.partial(kernel, nx, ny), out_shape=[pltpu.VMEM(s...  104 us
    pallas_call x1, Pallas kernels, shards(): pl.pallas_call(functools.partial(store_kernel, nx, ny), out_shape=[jax.Sh...  3.83 us

profile of v2, /device:TPU:6, one launch (start us, length us, event | category | flops | bytes accessed | tf_op | source)
XLA Modules:
  0.0 108.3 jit_solution(2619748732885578706)
XLA Ops:
  0.6 103.9 %shard_map.85 = (f32[2016,128]{1,0:T(8,128)S(1)}, f32[2016,128]{1,0:T(8,128)S(1)}, f32[2016,128]{1,0:T(8,128)S(1)}, f32[2016,128]{1,0:T(8,128)S(1)}, f32[2016,12...) custom-call(f32[3,32,32,128]{3,2,1,0:T(8,128)} %e_in.1, ...), custom_call_target="tpu_custom_call" | custom-call | tf_op jit(solution)/shard_map/pallas_call | solution.py:766
  104.5 3.8 %shard_map.86 = (f32[3,32,32,128]{3,2,1,0:T(8,128)}, f32[3,32,32,128]{3,2,1,0:T(8,128)}, f32[12,32,32,128]{3,2,1,0:T(8,128)}) custom-call(f32[2016,128]{1,0:T(8,128)S(1)} %get-tuple-element.21.refs_0_, f32[2016,128]{1,0:T(8,128)S(1)} %get-tuple-element.22.refs_1_, f32[2016,128]{1,0:T(8,128)S(1)} %get-tuple-element.23.refs_2_, ...), custom_call_target="tpu_custom_call" | custom-call | tf_op jit(solution)/shard_map/pallas_call | solution.py:777

commit v3 on v2

--- a/solution.py
+++ b/solution.py
@@ -17,11 +17,12 @@
 
 M = 4
 D = 2
-PXR = 24
+PXR = 32
+PXO = 8
 XO, XR = 5, 42
 YO, YP = 8, 48
 PYP = 24
-U = 4
+U, UA, UE = 4, 4, 8
 NA = 7
 Z_SLOTS = (1, 2, 7, 8)
 X_SLOTS = (3, 4, 9, 10)
@@ -33,8 +34,8 @@
 ENDS = D * LAYER
 EXTRA = ENDS + 2 * NA * 4
 FACE = EXTRA + 64
-CORNER_ROWS = ((0, 4), (4, 3), (7, 2), (9, 1))
-CORNER = NA * 10
+CORNER_ROWS = ((0, 4), (4, 2), (6, 1), (7, 1))
+CORNER = NA * 8
 EDGE = D * 4 * 16
 
 
@@ -58,7 +59,7 @@
     x_first, x_last = gx == 0, gx == nx - 1
     y_first, y_last = gy == 0, gy == ny - 1
     tile = lambda ref: ref.reshape(XR, YP, 128).at[pl.ds(XO, 32), pl.ds(YO, 32), :]
-    pxview = lambda ref: ref.reshape(PXR, YP, 128).at[pl.ds(4, 16), pl.ds(YO, 32), :]
+    pxview = lambda ref: ref.reshape(PXR, YP, 128).at[pl.ds(PXO, 16), pl.ds(YO, 32), :]
     pyrows = lambda ref: ref.reshape(XR, PYP, 128).at[pl.ds(XO, 32), pl.ds(4, 16), :]
     x_layer = jnp.where(x_first, 0, 16)
     y_layer = pl.multiple_of(jnp.where(y_first, 0, 16), 8)
@@ -221,11 +222,11 @@
 
     def clear_beside(i, c):
         for ref in PX:
-            for start in (0, 20 * YP):
+            for start in (0, (PXO + 16) * YP):
                 ref[pl.ds(pl.multiple_of(start + i * 8, 8), 8), :] = zeros
         return c
 
-    lax.fori_loop(0, 4 * YP // 8, clear_beside, 0)
+    lax.fori_loop(0, PXO * YP // 8, clear_beside, 0)
 
     for copy in loads:
         copy.wait()
@@ -252,11 +253,20 @@
             table = [jnp.where(bit, table[i + 1], table[i]) for i in range(0, len(table), 2)]
         return table[0]
 
-    def coefficients(base):
-        number = MF[pl.ds(base, 8), :].astype(jnp.int32)
-        bits = [(number & (1 << k)) != 0 for k in range(3)]
-        KP[pl.ds(base, 8), :] = choose(bits, keep_of)
-        DR[pl.ds(base, 8), :] = choose(bits, drive_of)
+    def coefficients(ref, table, bases):
+        for base in bases:
+            number = MF[pl.ds(base, 8), :].astype(jnp.int32)
+            bits = [(number & (1 << k)) != 0 for k in range(3)]
+            ref[pl.ds(base, 8), :] = choose(bits, table)
+
+    def all_coefficients(first, last, ys):
+        for ref, table in ((KP, keep_of), (DR, drive_of)):
+
+            def one(x, c, ref=ref, table=table):
+                coefficients(ref, table, [at(x, y) + zero for y in ys])
+                return c
+
+            lax.fori_loop(first, last, one, 0)
 
     at = lambda x, y: (x + XO) * YP + YO + y
 
@@ -265,10 +275,10 @@
             MF[pl.ds(at(x, 8 * k), 8), :] = MI[
                 pl.ds(pl.multiple_of(x * 32 + 8 * k, 8), 8), :
             ].astype(jnp.float32)
-            coefficients(at(x, 8 * k))
         return c
 
     lax.fori_loop(0, 32, own_material, 0)
+    all_coefficients(0, 32, (0, 8, 16, 24))
     pl.semaphore_wait(barrier, count)
 
     def remote(d, src, dst, ssem, rsem):
@@ -359,7 +369,7 @@
             x = i if dx < 0 else 31 - i
             rows = pl.ds(at(x, 0 if dy < 0 else 32 - n) + zero, n)
             for k, value in enumerate(gather(rows)):
-                buf[k * 10 + first : k * 10 + first + n, :] = value
+                buf[k * 8 + first : k * 8 + first + n, :] = value
         copy = remote(
             d, buf, recv_c[OPP[d] - 4].at[blk], s_sem.at[d, 0], r_sem.at[blk, OPP[d], 0]
         )
@@ -372,7 +382,7 @@
             place = -1 - layer if DIRS[d][d // 2] < 0 else 32 + layer
         if d < 2:
             return [pl.ds((place + XO) * PYP + 4 + 8 * q + zero, 8) for q in range(2)]
-        return [pl.ds((8 * q + 4) * YP + YO + place + zero, 8, stride=YP) for q in range(2)]
+        return [pl.ds((8 * q + PXO) * YP + YO + place + zero, 8, stride=YP) for q in range(2)]
 
     def send_edge(d, blk):
         @pl.when(jnp.logical_and(exists[d], y_edge if d < 2 else x_edge))
@@ -432,7 +442,7 @@
             copy.wait_send()
             for i, (first, n) in enumerate(CORNER_ROWS):
                 x = -1 - i if dx < 0 else 32 + i
-                s = lambda k: k * 10 + first
+                s = lambda k: k * 8 + first
                 scatter(
                     pl.ds(at(x, -n if dy < 0 else 32) + zero, n),
                     [buf[blk, s(k) : s(k) + n, :] for k in range(NA)],
@@ -498,29 +508,19 @@
                         rows = pl.ds(at(x, -4 if dy < 0 else 32) + zero, 4)
                         MF[rows, :] = recv_mc[d - 4][i * 4 : i * 4 + 4, :]
 
-        def whole_row(x, c):
-            for k in range(5):
-                coefficients(at(x, 8 * k - 4) + zero)
-            return c
-
-        def ends_of_row(x, c):
-            for k in (0, 4):
-                coefficients(at(x, 8 * k - 4) + zero)
-            return c
-
-        lax.fori_loop(-4, 0, whole_row, 0)
-        lax.fori_loop(32, 36, whole_row, 0)
-        lax.fori_loop(0, 32, ends_of_row, 0)
+        all_coefficients(-4, 0, (-4, 4, 12, 20, 28))
+        all_coefficients(32, 36, (-4, 4, 12, 20, 28))
+        all_coefficients(0, 32, (-4, 28))
 
     def table(tab, half, k, start, n):
         return tab[pl.ds(half * 3 * n + k * n + start, 8), :]
 
-    def half_step(half, x0, starts, mask_of, px, py):
+    def half_step(half, x0, size, starts, mask_of, px, py):
         source, target = (E, H) if half == 0 else (H, E)
         step = 1 if half == 0 else -1
         zc = [ztab[(half * 3 + k) * 8 : (half * 3 + k) * 8 + 8, :] for k in range(3)]
         keep_lane = lane < 127 if half == 0 else lane > 0
-        for r in range(U):
+        for r in range(size):
             x = x0 + r
             if px:
                 xc = [
@@ -556,7 +556,7 @@
                 tz1 = term(dz1, zc, PZ[2 * half], here)
                 tz0 = term(dz0, zc, PZ[2 * half + 1], here)
                 if px:
-                    there = pl.ds((x - pxbase + 4) * YP + YO + y + zero, 8)
+                    there = pl.ds((x - pxbase + PXO) * YP + YO + y + zero, 8)
                     tx2 = term(dx2, xc, PX[2 * half], there)
                     tx1 = term(dx1, xc, PX[2 * half + 1], there)
                 else:
@@ -582,14 +582,15 @@
     px0 = jnp.where(x_first, 0, jnp.where(x_last, 16, -32))
     px1 = jnp.where(x_edge, px0 + 16, -32)
 
-    def groups(half, xs, xe, starts, mask_of, py):
-        n = (xe - xs + U - 1) // U
-        ia = jnp.clip((px0 - xs + 64) // U - 64 // U, 0, n)
-        ib = jnp.clip((px1 - xs + 64 + U - 1) // U - 64 // U, 0, n)
+    def groups(half, xs, xe, size, starts, mask_of, py):
+        over = lambda v: (v + 64) // size - 64 // size
+        n = over(xe - xs + size - 1)
+        ia = jnp.clip(over(px0 - xs), 0, n)
+        ib = jnp.clip(over(px1 - xs + size - 1), 0, n)
 
         def plain(part, c):
             def one(i, c):
-                half_step(half, xs + U * i, starts, mask_of, False, py)
+                half_step(half, xs + size * i, size, starts, mask_of, False, py)
                 return c
 
             return lax.fori_loop(jnp.where(part == 0, 0, ib), jnp.where(part == 0, ia, n), one, c)
@@ -597,7 +598,7 @@
         lax.fori_loop(0, 2, plain, 0)
 
         def layered(i, c):
-            half_step(half, xs + U * i, starts, mask_of, True, py)
+            half_step(half, xs + size * i, size, starts, mask_of, True, py)
             return c
 
         lax.fori_loop(ia, ib, layered, 0)
@@ -637,9 +638,9 @@
                     return within(row + starts_a[i], ylo, jnp.where(ok > 0, yhi, -99))
                 return row >= 8 - 8 * ok
 
-            groups(half, xlo, xhi, starts_a, mask_of, py)
-
-    def pass_b(t, py):
+            groups(half, xlo, xhi, UA, starts_a, mask_of, py)
+
+    def pass_b(t):
         ya = jnp.where(y_first, 0, -99)
         yb = jnp.where(y_last, 32, 99)
         for half in range(2):
@@ -670,13 +671,16 @@
                     return within(y, wa, jnp.where(x < xe, yc, -99))
                 return within(y, yd, jnp.where(x < xe, wb, -99))
 
-            def border(p, c, half=half, low=low, high=high, mask_of=mask_of):
-                half_step(half, jnp.where(p == 0, low, high), starts_b, mask_of, False, py)
-                return c
-
-            lax.fori_loop(jnp.where(x_first, 1, 0), jnp.where(x_last, 1, 2), border, 0)
-            ends_py = {k // 4: v for k, v in py.items() if k in (0, 4)}
-            groups(half, xs, xe, (-4, 28), ends_mask, ends_py)
+            def borders(py, half=half, low=low, high=high, mask_of=mask_of):
+                def border(p, c):
+                    x0 = jnp.where(p == 0, low, high)
+                    half_step(half, x0, U, starts_b, mask_of, False, py)
+                    return c
+
+                lax.fori_loop(jnp.where(x_first, 1, 0), jnp.where(x_last, 1, 2), border, 0)
+
+            by_place(borders, (0, 1, 2), (2, 3, 4))
+            groups(half, xs, xe, UE, (-4, 28), ends_mask, {})
 
             def outside_mask(r, x, i, low=low, yc=yc, yd=yd, wa=wa, wb=wb):
                 y = row + (-4 if i == 0 else 28)
@@ -686,7 +690,7 @@
 
             @pl.when(jnp.logical_and(jnp.logical_not(x_first), low + 5 - t - half > 0))
             def _(half=half, outside_mask=outside_mask):
-                half_step(half, t - 5 + half, (-4, 28), outside_mask, False, ends_py)
+                half_step(half, t - 5 + half, U, (-4, 28), outside_mask, False, {})
 
     def block(turn, c):
         blk = turn % 2
@@ -699,6 +703,11 @@
 
             by_place(lambda py: pass_a(t, py), (0, 1), (2, 3))
 
+            @pl.when(t == D)
+            def _():
+                for d in range(4, 8):
+                    send_corner(d, blk)
+
             @pl.when(t <= D)
             def _():
                 send_layer(0, t - 1, blk)
@@ -708,8 +717,6 @@
             def _():
                 for d in range(4):
                     send_tail(d, blk)
-                for d in range(4, 8):
-                    send_corner(d, blk)
                 for d in range(4):
                     send_edge(d, blk)
 
@@ -729,7 +736,7 @@
             receive_face(d, blk)
 
         def step_b(t, c):
-            by_place(lambda py: pass_b(t, py), (0, 1, 2), (2, 3, 4))
+            pass_b(t)
             return c
 
         lax.fori_loop(1, M + 1, step_b, 0)

time: 108 us -> 100 us (0.926)
  Pallas kernels: 108 us -> 99.5 us
    pallas_call x1, Pallas kernels: 104 us -> 95.6 us  [shards(): pl.pallas_call(functools.partial(kernel, nx, ny), out_shape=[pltpu.VMEM(s...]
where the time goes in v3:
time: 100 us
  Pallas kernels  99.5 us (100%)
    pallas_call x1, Pallas kernels, shards(): pl.pallas_call(functools.partial(kernel, nx, ny), out_shape=[pltpu.VMEM(s...  95.6 us
    pallas_call x1, Pallas kernels, shards(): pl.pallas_call(functools.partial(store_kernel, nx, ny), out_shape=[jax.Sh...  3.83 us

profile of v3, /device:TPU:6, one launch (start us, length us, event | category | flops | bytes accessed | tf_op | source)
XLA Modules:
  0.0 100.1 jit_solution(14395624236356439181)
XLA Ops:
  0.6 95.6 %shard_map.85 = (f32[2016,128]{1,0:T(8,128)S(1)}, f32[2016,128]{1,0:T(8,128)S(1)}, f32[2016,128]{1,0:T(8,128)S(1)}, f32[2016,128]{1,0:T(8,128)S(1)}, f32[2016,12...) custom-call(f32[3,32,32,128]{3,2,1,0:T(8,128)} %e_in.1, ...), custom_call_target="tpu_custom_call" | custom-call | tf_op jit(solution)/shard_map/pallas_call | solution.py:773
  96.3 3.8 %shard_map.86 = (f32[3,32,32,128]{3,2,1,0:T(8,128)}, f32[3,32,32,128]{3,2,1,0:T(8,128)}, f32[12,32,32,128]{3,2,1,0:T(8,128)}) custom-call(f32[2016,128]{1,0:T(8,128)S(1)} %get-tuple-element.21.refs_0_, f32[2016,128]{1,0:T(8,128)S(1)} %get-tuple-element.22.refs_1_, f32[2016,128]{1,0:T(8,128)S(1)} %get-tuple-element.23.refs_2_, ...), custom_call_target="tpu_custom_call" | custom-call | tf_op jit(solution)/shard_map/pallas_call | solution.py:784
